TPU v7x, 16 devices: a 4x2x1 block of a 4x4x8 slice. The times are simulated.
16 devices in a mesh: rep: 2 (over y, z), dp: 8 (over x, core).
Axes of the slice: x: 4, y: 2, z: 1, core: 2. Of those that a mesh axis runs over, the one named last changes fastest.
The devices are a block of a 4x4x8 slice.
Arguments:
- x: bfloat16 [16, 2048, 1024], P(('rep', 'dp')), parts along dimension 0
- dy: bfloat16 [16, 2048, 1024], P(('rep', 'dp')), parts along dimension 0
- w_gate: bfloat16 [2, 1024, 2816], replicated
- w_up: bfloat16 [2, 1024, 2816], replicated
- w_down: bfloat16 [2, 2816, 1024], replicated
- m_w_gate: float32 [2, 1024, 2816], P(None, 'dp')
- m_w_up: float32 [2, 1024, 2816], P(None, 'dp')
- m_w_down: float32 [2, 2816, 1024], P(None, 'dp')
- v_w_gate: float32 [2, 1024, 2816], P(None, 'dp')
- v_w_up: float32 [2, 1024, 2816], P(None, 'dp')
- v_w_down: float32 [2, 2816, 1024], P(None, 'dp')
Outputs:
- output 1: bfloat16 [4, 1024, 2816], P('rep'), parts along dimension 0
- output 2: bfloat16 [4, 1024, 2816], P('rep'), parts along dimension 0
- output 3: bfloat16 [4, 2816, 1024], P('rep'), parts along dimension 0
- output 4: float32 [4, 1024, 2816], P('rep', 'dp'), parts along dimension 0
- output 5: float32 [4, 1024, 2816], P('rep', 'dp'), parts along dimension 0
- output 6: float32 [4, 2816, 1024], P('rep', 'dp'), parts along dimension 0
- output 7: float32 [4, 1024, 2816], P('rep', 'dp'), parts along dimension 0
- output 8: float32 [4, 1024, 2816], P('rep', 'dp'), parts along dimension 0
- output 9: float32 [4, 2816, 1024], P('rep', 'dp'), parts along dimension 0
There are 2 independent parts. A program takes and returns all parts, laid end to end along the dimension named above; an argument that names none is the same for every part.
All inputs are finite; a program needn't handle non-finite values.
Results may differ from a plain program's by a relative error of at most 0.022.
Values are sent between devices in bfloat16 or wider.
A program may use at most 768 MiB of HBM per device.

v0:
```python
import functools

import jax
import jax.numpy as jnp
from jax import lax
from jax.experimental import pallas as pl
from jax.experimental.pallas import tpu as pltpu
from jax.sharding import PartitionSpec as P

MESH = pl.DeviceIdType.MESH
F32, BF16 = jnp.float32, jnp.bfloat16
CORES = 2


def places(axis, n):
    me = lax.axis_index(axis)
    chips = n // CORES
    core, chip = lax.rem(me, CORES), lax.div(me, CORES)
    at = lambda away: lax.rem(chip + away, chips) * CORES + core
    return me, core, me + 1 - 2 * core, at(1), at(chips - 1), at(2)


def finish_kernel(n, count, pieces, *refs):
    g_in, w_in, m_in, v_in, w_out, m_out, v_out = (refs[3 * i : 3 * i + 3] for i in range(7))
    g, w, m, v, new = (refs[21 + 3 * i : 24 + 3 * i] for i in range(5))
    parts, load_sem, own_sem, store_sem, part_send, part_recv, send, recv = refs[36:]
    me, core, partner, after, before, across = places("dp", n)

    barrier = pltpu.get_barrier_semaphore()
    peers = [lax.rem(me + away, n) for away in range(1, n)]
    for peer in peers:
        pl.semaphore_signal(barrier, inc=1, device_id={"dp": peer}, device_id_type=MESH)

    loads = []
    for i in range(3):
        loads.append(pltpu.make_async_copy(g_in[i], g[i], load_sem.at[i]))
    for i in (2, 0, 1):
        rows = g[i].shape[1]
        mine = pl.ds(pl.multiple_of(me * rows, 16), rows)
        loads.append(pltpu.make_async_copy(w_in[i].at[:, mine], w[i], load_sem.at[3 + i]))
        loads.append(pltpu.make_async_copy(m_in[i], m[i], load_sem.at[6 + i]))
        loads.append(pltpu.make_async_copy(v_in[i], v[i], load_sem.at[9 + i]))
    for one in loads:
        one.start()

    total = jnp.zeros((8, 128), F32)
    for i in range(3):
        loads[i].wait()
        layers, rows, columns = g[i].shape

        def squares(step, total, ref=g[i], columns=columns, rows=rows):
            block = ref[lax.div(step, rows // 16), pl.ds(pl.multiple_of(lax.rem(step, rows // 16) * 16, 16), 16), :].astype(F32)
            block = block * block
            for at in range(0, columns, 128):
                total += block[:8, at : at + 128] + block[8:, at : at + 128]
            return total

        total = lax.fori_loop(0, layers * rows // 16, squares, total)
    parts[pl.ds(me, 1)] = total[None]
    pl.semaphore_wait(barrier, n - 1)
    part_copies = []
    for k, peer in enumerate(peers):
        part_copies.append(
            pltpu.make_async_remote_copy(
                parts.at[me], parts.at[me], part_send.at[k], part_recv.at[k], device_id={"dp": peer}, device_id_type=MESH
            )
        )
        part_copies[-1].start()
    for one in part_copies:
        one.wait_recv()
    every = parts[0]
    for k in range(1, n):
        every += parts[k]
    mean = jnp.sum(every, keepdims=True) / count
    factor = jnp.minimum(1.0, 0.5 * lax.rsqrt(mean + 1e-30))

    def adamw(i, layer, first, rows):
        step_rows = 16
        columns = g[i].shape[2]

        def body(step, _):
            at = (layer, pl.ds(pl.multiple_of(first + step * step_rows, 16), step_rows), slice(None))
            grad = g[i][at].astype(F32) * factor
            m_new = 0.9 * m[i][at] + 0.1 * grad
            v_new = 0.95 * v[i][at] + 0.05 * grad * grad
            w_old = w[i][at].astype(F32)
            m[i][at] = m_new
            v[i][at] = v_new
            new[i][at] = (w_old - 0.02 * (m_new * lax.rsqrt(v_new + 1e-8) + 0.1 * w_old)).astype(BF16)
            return 0

        lax.fori_loop(0, rows // step_rows, body, 0)

    def rows_of(i, owner, first, rows):
        return pl.ds(pl.multiple_of(owner * g[i].shape[1] + first, 16), rows)

    def remote(kind, number, src, dst, to):
        return pltpu.make_async_remote_copy(
            src, dst, send.at[kind, number], recv.at[kind, number], device_id={"dp": to}, device_id_type=MESH
        )

    def piece(number):
        i, layer, first, rows = pieces[number]
        place = lambda owner, columns=slice(None): w_out[i].at[layer, rows_of(i, owner, first, rows), columns]
        half = g[i].shape[2] // 2
        left, right = pl.ds(0, half), pl.ds(half, half)
        mine = new[i].at[layer, pl.ds(first, rows)]
        copies = {
            "after": remote(0, number, mine, place(me), after),
            "before": remote(1, number, mine, place(me), before),
            "partner": remote(2, number, mine, place(me), partner),
            "on": remote(3, number, place(before, left), place(before, left), after),
            "back": remote(4, number, place(after, right), place(after, right), before),
            "partner_before": remote(5, number, place(before), place(before), partner),
            "partner_after": remote(6, number, place(after), place(after), partner),
            "partner_left": remote(7, number, place(across, left), place(across, left), partner),
            "partner_right": remote(8, number, place(across, right), place(across, right), partner),
        }
        local = pltpu.make_async_copy(mine, place(me), own_sem.at[number])
        stores = [
            pltpu.make_async_copy(t[i].at[layer, pl.ds(first, rows)], o[i].at[layer, pl.ds(first, rows)], store_sem.at[k, number])
            for k, (t, o) in enumerate(((m, m_out), (v, v_out)))
        ]
        return copies, [local, *stores]

    waited = set()
    total_pieces = len(pieces)
    made = [piece(number) for number in range(total_pieces)]

    def compute(number):
        i, layer, first, rows = pieces[number]
        if i not in waited:
            waited.add(i)
            for one in loads[3 + 3 * (2, 0, 1).index(i) :][:3]:
                one.wait()
        adamw(i, layer, first, rows)

    compute(0)
    for number in range(total_pieces + 2):
        if number + 1 < total_pieces:
            compute(number + 1)
        if number < total_pieces:
            copies, local = made[number]
            for kind in ("after", "before", "partner"):
                copies[kind].start()
            for one in local:
                one.start()
        if 1 <= number <= total_pieces:
            copies, _ = made[number - 1]
            copies["after"].wait_recv()
            copies["on"].start()
            copies["partner_before"].start()
            copies["before"].wait_recv()
            copies["back"].start()
            copies["partner_after"].start()
        if 2 <= number:
            copies, _ = made[number - 2]
            copies["on"].wait_recv()
            copies["partner_left"].start()
            copies["back"].wait_recv()
            copies["partner_right"].start()
    for copies, local in made:
        for kind in ("partner", "partner_before", "partner_after", "partner_left", "partner_right"):
            copies[kind].wait_recv()
        for one in copies.values():
            one.wait_send()
        for one in local:
            one.wait()
    for one in part_copies:
        one.wait_send()


def finish(n, gradients, weights, m, v):
    count = float(sum(w.size for w in weights))
    pieces = []
    for i in (2, 0, 1):
        layers, rows, _ = gradients[i].shape
        for layer in range(layers):
            for half in range(2):
                pieces.append((i, layer, half * rows // 2, rows // 2))
    anywhere = pl.BlockSpec(memory_space=pl.ANY)
    shapes = [t.shape for t in gradients]
    of = lambda dtype: [pltpu.VMEM(s, dtype) for s in shapes]
    dma = pltpu.SemaphoreType.DMA
    return pl.pallas_call(
        functools.partial(finish_kernel, n, count, tuple(pieces)),
        out_shape=[jax.ShapeDtypeStruct(t.shape, t.dtype) for t in (*weights, *m, *v)],
        in_specs=[anywhere] * 12,
        out_specs=[anywhere] * 9,
        scratch_shapes=[
            *of(BF16), *of(BF16), *of(F32), *of(F32), *of(BF16),
            pltpu.VMEM((n, 8, 128), F32),
            dma((12,)), dma((len(pieces),)), dma((2, len(pieces))), dma((n - 1,)), dma((n - 1,)),
            dma((9, len(pieces))), dma((9, len(pieces))),
        ],
        compiler_params=pltpu.CompilerParams(collective_id=4, has_side_effects=True, vmem_limit_bytes=48 * 2**20),
        name="finish",
    )(*gradients, *weights, *m, *v)


def dot(a, b, contract=((1,), (0,))):
    return lax.dot_general(a, b, (contract, ((), ())), preferred_element_type=F32)


def normed(h):
    wide = h.astype(F32)
    return (wide * lax.rsqrt(jnp.mean(wide * wide, -1, keepdims=True) + 1e-6)).astype(BF16)


def by_norm(h, by_a):
    wide = h.astype(F32)
    scale = lax.rsqrt(jnp.mean(wide * wide, -1, keepdims=True) + 1e-6)
    return scale * by_a - wide * (scale * scale * scale * jnp.mean(by_a * wide, -1, keepdims=True))


def by_units(gate, up, by_hidden):
    by_hidden = by_hidden.astype(BF16).astype(F32)
    s = jax.nn.sigmoid(gate)
    silu = gate * s
    return silu * up, by_hidden * up * (s + silu * (1.0 - s)), by_hidden * silu


def forward_kernel(tiles, x, w_gate, w_up, w_down, gate_out, up_out, hidden_t, a_t, h_out, next_a, next_a_t, wg, wu, wd, sem):
    tile = pl.program_id(0)
    loads = [pltpu.make_async_copy(src.at[0], dst, sem.at[k]) for k, (src, dst) in enumerate(((w_gate, wg), (w_up, wu), (w_down, wd)))]

    @pl.when(tile == 0)
    def _():
        for one in loads:
            one.start()

    a = normed(x[...])
    a_t[...] = a.T

    @pl.when(tile == 0)
    def _():
        loads[0].wait()
        loads[1].wait()

    columns = wg.shape[1]
    width = 256
    hidden = []
    for at in range(0, columns, width):
        gate = dot(a, wg[:, at : at + width])
        up = dot(a, wu[:, at : at + width])
        gate_out[:, at : at + width] = gate
        up_out[:, at : at + width] = up
        hidden.append((gate * jax.nn.sigmoid(gate) * up).astype(BF16))
        hidden_t[at : at + width, :] = hidden[-1].T

    @pl.when(tile == 0)
    def _():
        loads[2].wait()

    h = x[...] + dot(jnp.concatenate(hidden, 1), wd[...]).astype(BF16)
    h_out[...] = h
    b = normed(h)
    next_a[...] = b
    next_a_t[...] = b.T


def layer_0(x, w_gate, w_up, w_down):
    tokens, d = x.shape
    ff = w_gate.shape[2]
    rows = 256
    anywhere = pl.BlockSpec(memory_space=pl.ANY)
    tall = lambda n: pl.BlockSpec((rows, n), lambda i: (i, 0))
    wide = lambda n: pl.BlockSpec((n, rows), lambda i: (0, i))
    return pl.pallas_call(
        functools.partial(forward_kernel, tokens // rows),
        grid=(tokens // rows,),
        in_specs=[tall(d), anywhere, anywhere, anywhere],
        out_specs=[tall(ff), tall(ff), wide(ff), wide(d), tall(d), tall(d), wide(d)],
        out_shape=[
            jax.ShapeDtypeStruct((tokens, ff), F32),
            jax.ShapeDtypeStruct((tokens, ff), F32),
            jax.ShapeDtypeStruct((ff, tokens), BF16),
            jax.ShapeDtypeStruct((d, tokens), BF16),
            jax.ShapeDtypeStruct((tokens, d), BF16),
            jax.ShapeDtypeStruct((tokens, d), BF16),
            jax.ShapeDtypeStruct((d, tokens), BF16),
        ],
        scratch_shapes=[pltpu.VMEM((d, ff), BF16), pltpu.VMEM((d, ff), BF16), pltpu.VMEM((ff, d), BF16), pltpu.SemaphoreType.DMA((3,))],
        compiler_params=pltpu.CompilerParams(vmem_limit_bytes=60 * 2**20),
        name="forward",
    )(x, w_gate, w_up, w_down)


SLOTS = 6
HELD = 4
SENT = 3


class Exchange:
    def __init__(self, n, refs, kinds):
        self.mine, self.pair, self.out2, self.out3, self.in2, self.in3, self.pair_sem, self.sem2, self.sem3 = refs
        self.kinds = kinds
        self.me, self.core, self.partner, self.after, self.before, _ = places("dp", n)
        chips = n // CORES
        chip = lax.div(self.me, CORES)
        self.chip = chip
        self.chip_after, self.chip_before, self.chip_across = (lax.rem(chip + k, chips) for k in (1, chips - 1, chips // 2))

    @staticmethod
    def scratch(n, rows, width):
        chips, half, dma = n // CORES, width // 2, pltpu.SemaphoreType.DMA
        return [
            pltpu.VMEM((HELD, chips, CORES, rows, width), BF16),
            pltpu.VMEM((SLOTS, chips, rows, width), BF16),
            pltpu.VMEM((2, SENT, rows, width), BF16),
            pltpu.VMEM((2, SENT, rows, half), BF16),
            pltpu.VMEM((2, SLOTS, rows, width), BF16),
            pltpu.VMEM((2, SLOTS, rows, half), BF16),
            dma((2, SLOTS)), dma((2, 2, SLOTS)), dma((2, 2, SLOTS)),
        ]

    def barrier(self):
        barrier = pltpu.get_barrier_semaphore()
        for peer in (self.partner, self.after, self.before):
            pl.semaphore_signal(barrier, inc=1, device_id={"dp": peer}, device_id_type=MESH)
        pl.semaphore_wait(barrier, 3)

    def copy1(self, p, rows):
        slot = lax.rem(p, SLOTS)
        return pltpu.make_async_remote_copy(
            self.mine.at[lax.rem(p, HELD), :, 1 - self.core, pl.ds(0, rows)], self.pair.at[slot, :, pl.ds(0, rows)],
            self.pair_sem.at[0, slot], self.pair_sem.at[1, slot], device_id={"dp": self.partner}, device_id_type=MESH,
        )

    def copies(self, p, rows, out, into, sem):
        slot = lax.rem(p, SLOTS)
        return [
            pltpu.make_async_remote_copy(
                out.at[way, lax.rem(p, SENT), pl.ds(0, rows)], into.at[way, slot, pl.ds(0, rows)],
                sem.at[0, way, slot], sem.at[1, way, slot], device_id={"dp": to}, device_id_type=MESH,
            )
            for way, to in enumerate((self.after, self.before))
        ]

    def over(self, rows, body):
        def step(i, _):
            body(pl.ds(pl.multiple_of(i * 16, 16), 16))
            return 0

        lax.fori_loop(0, rows // 16, step, 0)

    def of_chip(self, p, chip, at, columns):
        a = self.mine[lax.rem(p, HELD), chip, self.core, at, columns].astype(F32)
        return a + self.pair[lax.rem(p, SLOTS), chip, at, columns].astype(F32)

    def stage1(self, p, rows, _):
        self.copy1(p, rows).start()

    def stage2(self, p, rows, _):
        self.copy1(p, rows).wait()
        slot = lax.rem(p, SENT)
        half = self.out3.shape[-1]
        left, right = slice(0, half), slice(half, 2 * half)

        def body(at):
            self.out2[0, slot, at, left] = self.of_chip(p, self.chip_across, at, left).astype(BF16)
            self.out2[0, slot, at, right] = self.of_chip(p, self.chip_after, at, right).astype(BF16)
            self.out2[1, slot, at, left] = self.of_chip(p, self.chip_before, at, left).astype(BF16)
            self.out2[1, slot, at, right] = self.of_chip(p, self.chip_across, at, right).astype(BF16)

        self.over(rows, body)
        for one in self.copies(p, rows, self.out2, self.in2, self.sem2):
            one.start()

    def stage3(self, p, rows, _):
        for one in self.copies(p, rows, self.out2, self.in2, self.sem2):
            one.wait()
        slot, arrived = lax.rem(p, SENT), lax.rem(p, SLOTS)
        half = self.out3.shape[-1]
        left, right = slice(0, half), slice(half, 2 * half)

        def body(at):
            self.out3[0, slot, at] = (self.of_chip(p, self.chip_after, at, left) + self.in2[0, arrived, at, left].astype(F32)).astype(BF16)
            self.out3[1, slot, at] = (self.of_chip(p, self.chip_before, at, right) + self.in2[1, arrived, at, right].astype(F32)).astype(BF16)

        self.over(rows, body)
        for one in self.copies(p, rows, self.out3, self.in3, self.sem3):
            one.start()

    def stage4(self, p, rows, keep):
        for one in self.copies(p, rows, self.out3, self.in3, self.sem3):
            one.wait()
        arrived = lax.rem(p, SLOTS)
        half = self.out3.shape[-1]
        left, right = slice(0, half), slice(half, 2 * half)

        def body(at):
            a = self.of_chip(p, self.chip, at, left) + (self.in3[0, arrived, at].astype(F32) + self.in2[1, arrived, at, left].astype(F32))
            b = self.of_chip(p, self.chip, at, right) + (self.in2[0, arrived, at, right].astype(F32) + self.in3[1, arrived, at].astype(F32))
            keep(p, at, a.astype(BF16), b.astype(BF16))

        self.over(rows, body)

    def move(self, step, low, high):
        for lag, stage in enumerate((self.stage1, self.stage2, self.stage3, self.stage4)):
            for first, end, rows, keep in self.kinds:
                if high - 1 - lag < first or low - lag >= end:
                    continue
                p = step - lag
                if low - lag >= first and high - 1 - lag < end:
                    stage(p, rows, keep)
                else:
                    pl.when((p >= first) & (p < end))(functools.partial(stage, p, rows, keep))


def keep_columns(first, gate, up, width):
    def keep(p, at, left, right):
        columns = pl.ds(pl.multiple_of((p - first) * width, width), width)
        gate[at, columns] = left
        up[at, columns] = right

    return keep


def keep_down(first, down, rows, width):
    def keep(p, at, left, right):
        half = width // 2
        which = p - first
        at = pl.ds(pl.multiple_of(lax.rem(which, 2) * rows + at.start, 16), at.size)
        start = lax.div(which, 2) * width
        down[at, pl.ds(pl.multiple_of(start, half), half)] = left
        down[at, pl.ds(pl.multiple_of(start + half, half), half)] = right

    return keep


def down_packet(exchange, step, first, hidden_t, by_out):
    n_rows = hidden_t.shape[0]
    _, chips, cores, rows, width = exchange.mine.shape
    which = step - first
    start = pl.multiple_of(lax.rem(which, 2) * rows, 16)
    columns = pl.ds(pl.multiple_of(lax.div(which, 2) * width, width), width)
    share = n_rows // (chips * cores)
    lhs = jnp.concatenate([hidden_t[pl.ds(pl.multiple_of(k * share + start, 16), rows), :] for k in range(chips * cores)], 0)
    block = dot(lhs, by_out[:, columns]).astype(BF16)
    exchange.mine[lax.rem(step, HELD)] = block.reshape(chips, cores, rows, width)


def wide_packet(exchange, step, a_t, by_both):
    _, chips, cores, _, width = exchange.mine.shape
    rows = a_t.shape[0] // (chips * cores)
    half = width // 2
    for k in range(2):
        columns = slice(k * half, k * half + half)
        block = dot(a_t[...], by_both[:, columns]).astype(BF16)
        exchange.mine[lax.rem(step, HELD), :, :, pl.ds(0, rows), columns] = block.reshape(chips, cores, rows, half)


MB = 512


def top_kernel(n, *refs):
    (a_in, at_in, h_in, dy_in, w_gate, w_up, w_down), refs = refs[:7], refs[7:]
    (g_gate, g_up, g_down, by_h, bg_hbm, bu_hbm), refs = refs[:6], refs[6:]
    (a, a_t, dy, wg, wu, hidden_t, wd, both, h_tile, by_tile, load_sem, wd_sem, both_sem, tile_sem, by_sem), refs = refs[:15], refs[15:]
    tokens, d = a.shape
    ff = wg.shape[1]
    width = 256
    chunks = ff // width
    downs = 4
    wide_rows, down_rows = d // n, ff // n // 2
    exchange = Exchange(
        n, refs,
        (
            (0, chunks, wide_rows, keep_columns(0, g_gate, g_up, width)),
            (chunks, chunks + downs, down_rows, keep_down(chunks, g_down, down_rows, 2 * width)),
        ),
    )
    layer = w_gate.shape[0] - 1
    first, rest = pl.ds(0, width), pl.ds(width, ff - width)
    loads = [
        pltpu.make_async_copy(a_in, a, load_sem.at[0]),
        pltpu.make_async_copy(w_gate.at[layer, :, first], wg.at[:, first], load_sem.at[1]),
        pltpu.make_async_copy(w_up.at[layer, :, first], wu.at[:, first], load_sem.at[2]),
        pltpu.make_async_copy(dy_in, dy, load_sem.at[3]),
        pltpu.make_async_copy(at_in, a_t, load_sem.at[4]),
        pltpu.make_async_copy(w_gate.at[layer, :, rest], wg.at[:, rest], load_sem.at[5]),
        pltpu.make_async_copy(w_up.at[layer, :, rest], wu.at[:, rest], load_sem.at[6]),
    ]

    def down_chunk(c):
        slot = lax.rem(c, 2)
        return pltpu.make_async_copy(w_down.at[layer, pl.ds(pl.multiple_of(c * width, width), width)], wd.at[slot], wd_sem.at[slot])

    for one in loads[:4]:
        one.start()
    down_chunk(0).start()
    for one in loads[4:]:
        one.start()
    exchange.barrier()

    def store_both(c, k):
        slot = lax.rem(c, 2)
        return pltpu.make_async_copy(
            both.at[slot, :, pl.ds(k * width, width)],
            (bg_hbm, bu_hbm)[k].at[:, pl.ds(pl.multiple_of(c * width, width), width)],
            both_sem.at[k, slot],
        )

    def chunk(c, _):
        slot = lax.rem(c, 2)

        @pl.when(c == 0)
        def _():
            for one in loads[:5]:
                one.wait()

        @pl.when(c == 1)
        def _():
            for one in loads[5:]:
                one.wait()

        @pl.when(c >= 2)
        def _():
            for k in range(2):
                store_both(c - 2, k).wait()

        down_chunk(c).wait()

        @pl.when(c + 1 < chunks)
        def _():
            down_chunk(c + 1).start()

        columns = pl.ds(pl.multiple_of(c * width, width), width)
        wg_c, wu_c, wd_c = wg[:, columns], wu[:, columns], wd[slot]
        for at in range(0, tokens, MB):
            rows = slice(at, at + MB)
            hidden, by_gate, by_up = by_units(dot(a[rows], wg_c), dot(a[rows], wu_c), dot(dy[rows], wd_c, ((1,), (1,))))
            hidden_t[columns, rows] = hidden.astype(BF16).T
            both[slot, rows, :width] = by_gate.astype(BF16)
            both[slot, rows, width:] = by_up.astype(BF16)
        wide_packet(exchange, c, a_t, both.at[slot])
        for k in range(2):
            store_both(c, k).start()
        exchange.move(c, 0, chunks)
        return 0

    lax.fori_loop(0, chunks, chunk, 0)
    for c in (chunks - 2, chunks - 1):
        for k in range(2):
            store_both(c, k).wait()

    tile_rows = 256
    tiles = tokens // tile_rows
    split = a_t.shape[1]

    def tile_loads(t):
        slot = lax.rem(t, 2)
        rows = pl.ds(pl.multiple_of(t * tile_rows, tile_rows), tile_rows)
        got = []
        for k, src in enumerate((bg_hbm, bu_hbm)):
            to = pl.ds(pl.multiple_of((slot * 2 + k) * tile_rows, tile_rows), tile_rows)
            got.append(pltpu.make_async_copy(src.at[rows, pl.ds(0, split)], a_t.at[to], tile_sem.at[2 * k, slot]))
            got.append(pltpu.make_async_copy(src.at[rows, pl.ds(split, ff - split)], a.at[to, pl.ds(0, ff - split)], tile_sem.at[2 * k + 1, slot]))
        got.append(pltpu.make_async_copy(h_in.at[rows], h_tile.at[slot], tile_sem.at[4, slot]))
        return got

    def tile_store(t):
        slot = lax.rem(t, 2)
        return pltpu.make_async_copy(by_tile.at[slot], by_h.at[pl.ds(pl.multiple_of(t * tile_rows, tile_rows), tile_rows)], by_sem.at[slot])

    for one in tile_loads(0):
        one.start()

    def down(step, _):
        down_packet(exchange, step, chunks, hidden_t, dy)
        exchange.move(step, chunks, chunks + downs)
        return 0

    lax.fori_loop(chunks, chunks + downs, down, 0)

    def tile(step, _):
        t = step - chunks - downs
        slot = lax.rem(t, 2)
        for one in tile_loads(t):
            one.wait()

        @pl.when(t + 1 < tiles)
        def _():
            for one in tile_loads(t + 1):
                one.start()

        @pl.when(t >= 2)
        def _():
            tile_store(t - 2).wait()

        total = None
        for k, w in enumerate((wg, wu)):
            at = pl.ds(pl.multiple_of((slot * 2 + k) * tile_rows, tile_rows), tile_rows)
            term = dot(a_t[at], w[:, :split], ((1,), (1,))) + dot(a[at, : ff - split], w[:, split:], ((1,), (1,)))
            total = term if total is None else total + term
        rows = pl.ds(pl.multiple_of(t * tile_rows, tile_rows), tile_rows)
        by_tile[slot] = (dy[rows].astype(F32) + by_norm(h_tile[slot], total)).astype(BF16)
        tile_store(t).start()
        exchange.move(step, chunks + downs, chunks + downs + tiles)
        return 0

    lax.fori_loop(chunks + downs, chunks + downs + tiles, tile, 0)
    for t in (tiles - 2, tiles - 1):
        tile_store(t).wait()


def top_layer(n, a, a_t, h, dy, w_gate, w_up, w_down):
    tokens, d = a.shape
    ff = w_gate.shape[2]
    width = 256
    anywhere, inside = pl.BlockSpec(memory_space=pl.ANY), pl.BlockSpec(memory_space=pltpu.VMEM)
    dma = pltpu.SemaphoreType.DMA
    return pl.pallas_call(
        functools.partial(top_kernel, n),
        in_specs=[anywhere] * 7,
        out_specs=[inside] * 3 + [anywhere] * 3,
        out_shape=[
            jax.ShapeDtypeStruct((d // n, ff), BF16),
            jax.ShapeDtypeStruct((d // n, ff), BF16),
            jax.ShapeDtypeStruct((ff // n, d), BF16),
            jax.ShapeDtypeStruct((tokens, d), BF16),
            jax.ShapeDtypeStruct((tokens, ff), BF16),
            jax.ShapeDtypeStruct((tokens, ff), BF16),
        ],
        scratch_shapes=[
            pltpu.VMEM((tokens, d), BF16), pltpu.VMEM((d, tokens), BF16), pltpu.VMEM((tokens, d), BF16),
            pltpu.VMEM((d, ff), BF16), pltpu.VMEM((d, ff), BF16), pltpu.VMEM((ff, tokens), BF16),
            pltpu.VMEM((2, width, d), BF16), pltpu.VMEM((2, tokens, 2 * width), BF16),
            pltpu.VMEM((2, 256, d), BF16), pltpu.VMEM((2, 256, d), BF16),
            dma((7,)), dma((2,)), dma((2, 2)), dma((5, 2)), dma((2,)),
            *Exchange.scratch(n, ff // n // 2, 2 * width),
        ],
        compiler_params=pltpu.CompilerParams(collective_id=2, has_side_effects=True, vmem_limit_bytes=67043328),
        name="top",
    )(a, a_t, h, dy, w_gate, w_up, w_down)


def bottom_kernel(n, *refs):
    (by_in, ht_in, at_in, gate_in, up_in, w_down), refs = refs[:6], refs[6:]
    (g_gate, g_up, g_down), refs = refs[:3], refs[3:]
    (by, hidden_t, a_t, wd, gate, up, both, load_sem, wd_sem, unit_sem), refs = refs[:10], refs[10:]
    tokens, d = by.shape
    ff = hidden_t.shape[0]
    width = 256
    chunks = ff // width
    downs = 4
    wide_rows, down_rows = d // n, ff // n // 2
    exchange = Exchange(
        n, refs,
        (
            (0, downs, down_rows, keep_down(0, g_down, down_rows, 2 * width)),
            (downs, downs + chunks, wide_rows, keep_columns(downs, g_gate, g_up, width)),
        ),
    )
    loads = [
        pltpu.make_async_copy(ht_in, hidden_t, load_sem.at[0]),
        pltpu.make_async_copy(by_in, by, load_sem.at[1]),
        pltpu.make_async_copy(at_in, a_t, load_sem.at[2]),
    ]

    def chunk_loads(c):
        slot = lax.rem(c, 2)
        columns = pl.ds(pl.multiple_of(c * width, width), width)
        return [
            pltpu.make_async_copy(w_down.at[0, columns], wd.at[slot], wd_sem.at[slot]),
            pltpu.make_async_copy(gate_in.at[:, columns], gate.at[slot], unit_sem.at[0, slot]),
            pltpu.make_async_copy(up_in.at[:, columns], up.at[slot], unit_sem.at[1, slot]),
        ]

    for one in (*loads, *chunk_loads(0)):
        one.start()
    exchange.barrier()
    for one in loads[:2]:
        one.wait()

    def down(step, _):
        down_packet(exchange, step, 0, hidden_t, by)
        exchange.move(step, 0, downs)
        return 0

    lax.fori_loop(0, downs, down, 0)
    loads[2].wait()

    def chunk(step, _):
        c = step - downs
        slot = lax.rem(c, 2)
        for one in chunk_loads(c):
            one.wait()

        @pl.when(c + 1 < chunks)
        def _():
            for one in chunk_loads(c + 1):
                one.start()

        wd_c = wd[slot]
        for at in range(0, tokens, MB):
            rows = slice(at, at + MB)
            _, by_gate, by_up = by_units(gate[slot, rows], up[slot, rows], dot(by[rows], wd_c, ((1,), (1,))))
            both[rows, :width] = by_gate.astype(BF16)
            both[rows, width:] = by_up.astype(BF16)
        wide_packet(exchange, step, a_t, both)
        exchange.move(step, downs, downs + chunks)
        return 0

    lax.fori_loop(downs, downs + chunks, chunk, 0)
    for step in range(downs + chunks, downs + chunks + 3):
        exchange.move(step, step, step + 1)


def bottom_layer(n, by, hidden_t, a_t, gate, up, w_down):
    tokens, d = by.shape
    ff = hidden_t.shape[0]
    width = 256
    anywhere, inside = pl.BlockSpec(memory_space=pl.ANY), pl.BlockSpec(memory_space=pltpu.VMEM)
    dma = pltpu.SemaphoreType.DMA
    return pl.pallas_call(
        functools.partial(bottom_kernel, n),
        in_specs=[anywhere] * 6,
        out_specs=[inside] * 3,
        out_shape=[
            jax.ShapeDtypeStruct((d // n, ff), BF16),
            jax.ShapeDtypeStruct((d // n, ff), BF16),
            jax.ShapeDtypeStruct((ff // n, d), BF16),
        ],
        scratch_shapes=[
            pltpu.VMEM((tokens, d), BF16), pltpu.VMEM((ff, tokens), BF16), pltpu.VMEM((d, tokens), BF16),
            pltpu.VMEM((2, width, d), BF16), pltpu.VMEM((2, tokens, width), F32), pltpu.VMEM((2, tokens, width), F32),
            pltpu.VMEM((tokens, 2 * width), BF16),
            dma((3,)), dma((2,)), dma((2, 2)),
            *Exchange.scratch(n, ff // n // 2, 2 * width),
        ],
        compiler_params=pltpu.CompilerParams(collective_id=3, has_side_effects=True, vmem_limit_bytes=67043328),
        name="bottom",
    )(by, hidden_t, a_t, gate, up, w_down)


def solution(mesh):
    n = mesh.shape["dp"]

    def step(x, dy, w_gate, w_up, w_down, *moments):
        gate, up, hidden_t, a_t, h, next_a, next_a_t = layer_0(x[0], w_gate, w_up, w_down)
        *top, by_h, _, _ = top_layer(n, next_a, next_a_t, h, dy[0], w_gate, w_up, w_down)
        bottom = bottom_layer(n, by_h, hidden_t, a_t, gate, up, w_down)
        gradients = [jnp.stack(pair) for pair in zip(bottom, top, strict=True)]
        return tuple(finish(n, gradients, (w_gate, w_up, w_down), moments[:3], moments[3:]))

    sharded = P(None, "dp", None)
    return jax.shard_map(
        step,
        mesh=mesh,
        in_specs=(P(("rep", "dp")), P(("rep", "dp")), P(), P(), P(), *[sharded] * 6),
        out_specs=(*[P("rep")] * 3, *[P("rep", "dp")] * 6),
        check_vma=False,
    )
```

profile of v0, /device:TPU:113, one launch (start us, length us, event | category | flops | bytes accessed | tf_op | source)
XLA Modules:
  0.0 480.7 jit_solution(15573264253863453712)
XLA Ops:
  0.6 52.0 %forward.1 = (f32[2048,2816]{1,0:T(8,128)}, f32[2048,2816]{1,0:T(8,128)}, bf16[2816,2048]{1,0:T(8,128)(2,1)}, bf16[1024,2048]{1,0:T(8,128)(2,1)}, bf16[2048,1024...) custom-call(bf16[2048,1024]{1,0:T(8,128)(2,1)} %bitcast.10, bf16[2,1024,2816]{2,1,0:T(8,128)(2,1)} %refs_3_.1, ...), custom_call_target="tpu_custom_call" | custom-call | tf_op jit(solution)/shard_map/forward/pallas_call | solution.py:269
  52.6 134.4 %top.1 = (bf16[128,2816]{1,0:T(8,128)(2,1)}, bf16[128,2816]{1,0:T(8,128)(2,1)}, bf16[352,1024]{1,0:T(8,128)(2,1)}, bf16[2048,1024]{1,0:T(8,128)(2,1)}, bf16[2048...) custom-call(bf16[2048,1024]{1,0:T(8,128)(2,1)} %get-tuple-element.23.refs_0_, ...), custom_call_target="tpu_custom_call" | custom-call | tf_op jit(solution)/shard_map/top/pallas_call | solution.py:614
  187.0 95.4 %bottom.1 = (bf16[128,2816]{1,0:T(8,128)(2,1)}, bf16[128,2816]{1,0:T(8,128)(2,1)}, bf16[352,1024]{1,0:T(8,128)(2,1)}) custom-call(bf16[2048,1024]{1,0:T(8,128)(2,1)} %get-tuple-element.26.refs_0_, bf16[2816,2048]{1,0:T(8,128)(2,1)} %get-tuple-element.27.refs_1_, bf16[1024,2048]{1,0:T(8,128)(2,1)} %get-tuple-element.28.refs_2_, ...), custom_call_target="tpu_custom_call" | custom-call | tf_op jit(solution)/shard_map/bottom/pallas_call | solution.py:717
  282.4 2.1 pad_maximum_fusion
  284.6 0.0 copy-done.8
  284.6 0.1 pad_maximum_fusion.2.refs_2_
  284.8 155.6 %finish.1 = (bf16[2,1024,2816]{2,1,0:T(8,128)(2,1)}, bf16[2,1024,2816]{2,1,0:T(8,128)(2,1)}, bf16[2,2816,1024]{2,1,0:T(8,128)(2,1)}, f32[2,128,2816]{2,1,0:T(8,1...) custom-call(bf16[2,128,2816]{2,1,0:T(8,128)(2,1)S(1)} %get-tuple-ele, ...), custom_call_target="tpu_custom_call" | custom-call | tf_op jit(solution)/shard_map/finish/pallas_call | solution.py:185
  440.4 0.0 slice-start
  440.4 11.7 %copy.29 = bf16[2,1024,2816]{2,1,0:T(8,128)(2,1)} copy(bf16[2,1024,2816]{2,1,0:T(8,128)(2,1)} %get-tuple-element.48) | data formatting | bytes 23068672
  452.1 5.8 %copy.30 = bf16[2,1024,2816]{2,1,0:T(8,128)(2,1)} copy(bf16[2,1024,2816]{2,1,0:T(8,128)(2,1)S(1)} %copy-done) | data formatting | bytes 23068672
  458.0 0.7 slice-done.1
  458.6 1.3 slice-done.2
  460.0 4.8 %copy.31 = bf16[2,2816,1024]{2,1,0:T(8,128)(2,1)} copy(bf16[2,2816,1024]{2,1,0:T(8,128)(2,1)S(1)} %bitcast.9) | data formatting | bytes 23068672
  464.8 1.6 copy.32
  466.4 1.3 copy-done.5
  467.7 1.6 copy.33
  469.2 1.3 copy-done.4
  470.5 1.6 copy.34
  472.1 1.3 copy-done.3
  473.4 1.6 copy.35
  475.0 1.3 copy-done.2
  476.2 1.6 copy.36
  477.8 1.3 copy-done.1
  479.1 1.6 copy.37
  (16 shorter events, 0.0 us)
Async XLA Ops:
  282.4 2.1 copy-start.7
  282.4 2.2 copy-start.8
  440.4 11.7 %copy-start = (bf16[2,1024,2816]{2,1,0:T(8,128)(2,1)S(1)}, bf16[2,1024,2816]{2,1,0:T(8,128)(2,1)}, u32[]{:S(2)}) copy-start(bf16[2,1024,2816]{2,1,0:T(8,128)(2,1)} %get-tuple-element.49) | copy-start | bytes 34603012
  440.4 17.6 %slice-start = ((s8[11534336]{0:T(1024)(128)(4,1)}), s8[4194304]{0:T(1024)(128)(4,1)S(1)}, s32[]{:S(2)}) async-start(s8[11534336]{0:T(1024)(128)(4,1)} %bitcast.8), calls=%async_computation | async-start | bytes 8388608
  440.4 18.2 %slice-start.1 = ((s8[11534336]{0:T(1024)(128)(4,1)}), s8[4194304]{0:T(1024)(128)(4,1)S(1)}, s32[]{:S(2)}) async-start(s8[11534336]{0:T(1024)(128)(4,1)} %bitcast.8), calls=%async_computation.1 | async-start | bytes 8388608
  452.1 7.8 %slice-start.2 = ((s8[11534336]{0:T(1024)(128)(4,1)}), s8[3145728]{0:T(1024)(128)(4,1)S(1)}, s32[]{:S(2)}) async-start(s8[11534336]{0:T(1024)(128)(4,1)} %bitcast.8), calls=%async_computation.2 | async-start | bytes 6291456
  459.9 4.9 %copy-start.6 = (f32[2,128,2816]{2,1,0:T(8,128)S(1)}, f32[2,128,2816]{2,1,0:T(8,128)}, u32[]{:S(2)}) copy-start(f32[2,128,2816]{2,1,0:T(8,128)} %get-tuple-element.51) | copy-start | bytes 8650756
  464.8 2.9 copy-start.5
  467.7 2.9 copy-start.4
  470.5 2.9 copy-start.3
  473.4 2.9 copy-start.2
  476.2 2.9 copy-start.1
where the time goes:
time: 481 us
  Pallas kernels  437 us (91%)
  local copies, waits for them, and re-layouts  40.3 us (8%)
    pallas_call x1, Pallas kernels, finish(): pl.pallas_call(functools.partial(finish_kernel, n, count, tuple(pieces)),...  156 us
    pallas_call x1, Pallas kernels, top_layer(): pl.pallas_call(functools.partial(top_kernel, n), in_specs=[anywhere] * 7,...  134 us
    pallas_call x1, Pallas kernels, bottom_layer(): pl.pallas_call(functools.partial(bottom_kernel, n), in_specs=[anywhere] *...  95.4 us
    pallas_call x1, Pallas kernels, layer_0(): pl.pallas_call(functools.partial(forward_kernel, tokens // rows), grid=(t...  52 us
    unnamed x33, local copies, waits for them, and re-layouts  40.3 us

commit v1 on v0

--- a/solution.py
+++ b/solution.py
@@ -21,9 +21,11 @@
 
 
 def finish_kernel(n, count, pieces, *refs):
-    g_in, w_in, m_in, v_in, w_out, m_out, v_out = (refs[3 * i : 3 * i + 3] for i in range(7))
-    g, w, m, v, new = (refs[21 + 3 * i : 24 + 3 * i] for i in range(5))
-    parts, load_sem, own_sem, store_sem, part_send, part_recv, send, recv = refs[36:]
+    layers = 2
+    g_in, refs = [refs[layers * i : layers * i + layers] for i in range(3)], refs[3 * layers :]
+    w_in, m_in, v_in, w, m, v = (refs[3 * i : 3 * i + 3] for i in range(6))
+    g, refs = refs[18:21], refs[21:]
+    parts, load_sem, part_send, part_recv, send, recv = refs
     me, core, partner, after, before, across = places("dp", n)
 
     barrier = pltpu.get_barrier_semaphore()
@@ -31,29 +33,37 @@
     for peer in peers:
         pl.semaphore_signal(barrier, inc=1, device_id={"dp": peer}, device_id_type=MESH)
 
-    loads = []
-    for i in range(3):
-        loads.append(pltpu.make_async_copy(g_in[i], g[i], load_sem.at[i]))
-    for i in (2, 0, 1):
-        rows = g[i].shape[1]
-        mine = pl.ds(pl.multiple_of(me * rows, 16), rows)
-        loads.append(pltpu.make_async_copy(w_in[i].at[:, mine], w[i], load_sem.at[3 + i]))
-        loads.append(pltpu.make_async_copy(m_in[i], m[i], load_sem.at[6 + i]))
-        loads.append(pltpu.make_async_copy(v_in[i], v[i], load_sem.at[9 + i]))
-    for one in loads:
+    def rows_of(i, owner, first, rows):
+        return pl.ds(pl.multiple_of(owner * g[i].shape[1] + first, 16), rows)
+
+    order = (2, 0, 1)
+    g_loads = [[pltpu.make_async_copy(g_in[i][k], g[i].at[k], load_sem.at[layers * i + k]) for k in range(layers)] for i in order]
+    loads = {}
+    at = 3 * layers
+    for i in order:
+        rows = rows_of(i, me, 0, g[i].shape[1])
+        loads[i] = [
+            pltpu.make_async_copy(w_in[i].at[:, rows], w[i].at[:, rows], load_sem.at[at]),
+            pltpu.make_async_copy(m_in[i], m[i], load_sem.at[at + 1]),
+            pltpu.make_async_copy(v_in[i], v[i], load_sem.at[at + 2]),
+        ]
+        at += 3
+    for one in (*sum(g_loads, []), *sum((loads[i] for i in order), [])):
         one.start()
 
     total = jnp.zeros((8, 128), F32)
-    for i in range(3):
-        loads[i].wait()
-        layers, rows, columns = g[i].shape
+    for i, its_loads in zip(order, g_loads, strict=True):
+        _, rows, columns = g[i].shape
+        for one in its_loads:
+            one.wait()
 
         def squares(step, total, ref=g[i], columns=columns, rows=rows):
             block = ref[lax.div(step, rows // 16), pl.ds(pl.multiple_of(lax.rem(step, rows // 16) * 16, 16), 16), :].astype(F32)
             block = block * block
-            for at in range(0, columns, 128):
-                total += block[:8, at : at + 128] + block[8:, at : at + 128]
-            return total
+            sums = [block[:8, at : at + 128] + block[8:, at : at + 128] for at in range(0, columns, 128)]
+            while len(sums) > 1:
+                sums = [a + b for a, b in zip(sums[::2], sums[1::2])] + ([sums[-1]] if len(sums) % 2 else [])
+            return total + sums[0]
 
         total = lax.fori_loop(0, layers * rows // 16, squares, total)
     parts[pl.ds(me, 1)] = total[None]
@@ -76,52 +86,44 @@
 
     def adamw(i, layer, first, rows):
         step_rows = 16
-        columns = g[i].shape[2]
 
         def body(step, _):
-            at = (layer, pl.ds(pl.multiple_of(first + step * step_rows, 16), step_rows), slice(None))
+            start = first + step * step_rows
+            at = (layer, pl.ds(pl.multiple_of(start, 16), step_rows), slice(None))
+            mine = (layer, rows_of(i, me, start, step_rows), slice(None))
             grad = g[i][at].astype(F32) * factor
             m_new = 0.9 * m[i][at] + 0.1 * grad
             v_new = 0.95 * v[i][at] + 0.05 * grad * grad
-            w_old = w[i][at].astype(F32)
+            w_old = w[i][mine].astype(F32)
             m[i][at] = m_new
             v[i][at] = v_new
-            new[i][at] = (w_old - 0.02 * (m_new * lax.rsqrt(v_new + 1e-8) + 0.1 * w_old)).astype(BF16)
+            w[i][mine] = (w_old - 0.02 * (m_new * lax.rsqrt(v_new + 1e-8) + 0.1 * w_old)).astype(BF16)
             return 0
 
         lax.fori_loop(0, rows // step_rows, body, 0)
-
-    def rows_of(i, owner, first, rows):
-        return pl.ds(pl.multiple_of(owner * g[i].shape[1] + first, 16), rows)
-
-    def remote(kind, number, src, dst, to):
-        return pltpu.make_async_remote_copy(
-            src, dst, send.at[kind, number], recv.at[kind, number], device_id={"dp": to}, device_id_type=MESH
-        )
 
     def piece(number):
         i, layer, first, rows = pieces[number]
-        place = lambda owner, columns=slice(None): w_out[i].at[layer, rows_of(i, owner, first, rows), columns]
         half = g[i].shape[2] // 2
         left, right = pl.ds(0, half), pl.ds(half, half)
-        mine = new[i].at[layer, pl.ds(first, rows)]
-        copies = {
-            "after": remote(0, number, mine, place(me), after),
-            "before": remote(1, number, mine, place(me), before),
-            "partner": remote(2, number, mine, place(me), partner),
-            "on": remote(3, number, place(before, left), place(before, left), after),
-            "back": remote(4, number, place(after, right), place(after, right), before),
-            "partner_before": remote(5, number, place(before), place(before), partner),
-            "partner_after": remote(6, number, place(after), place(after), partner),
-            "partner_left": remote(7, number, place(across, left), place(across, left), partner),
-            "partner_right": remote(8, number, place(across, right), place(across, right), partner),
+
+        def copy(kind, to, owner, columns=slice(None)):
+            place = w[i].at[layer, rows_of(i, owner, first, rows), columns]
+            return pltpu.make_async_remote_copy(
+                place, place, send.at[kind, number], recv.at[kind, number], device_id={"dp": to}, device_id_type=MESH
+            )
+
+        return {
+            "after": copy(0, after, me),
+            "before": copy(1, before, me),
+            "partner": copy(2, partner, me),
+            "on": copy(3, after, before, left),
+            "back": copy(4, before, after, right),
+            "partner_before": copy(5, partner, before),
+            "partner_after": copy(6, partner, after),
+            "partner_left": copy(7, partner, across, left),
+            "partner_right": copy(8, partner, across, right),
         }
-        local = pltpu.make_async_copy(mine, place(me), own_sem.at[number])
-        stores = [
-            pltpu.make_async_copy(t[i].at[layer, pl.ds(first, rows)], o[i].at[layer, pl.ds(first, rows)], store_sem.at[k, number])
-            for k, (t, o) in enumerate(((m, m_out), (v, v_out)))
-        ]
-        return copies, [local, *stores]
 
     waited = set()
     total_pieces = len(pieces)
@@ -131,7 +133,7 @@
         i, layer, first, rows = pieces[number]
         if i not in waited:
             waited.add(i)
-            for one in loads[3 + 3 * (2, 0, 1).index(i) :][:3]:
+            for one in loads[i]:
                 one.wait()
         adamw(i, layer, first, rows)
 
@@ -140,13 +142,10 @@
         if number + 1 < total_pieces:
             compute(number + 1)
         if number < total_pieces:
-            copies, local = made[number]
             for kind in ("after", "before", "partner"):
-                copies[kind].start()
-            for one in local:
-                one.start()
+                made[number][kind].start()
         if 1 <= number <= total_pieces:
-            copies, _ = made[number - 1]
+            copies = made[number - 1]
             copies["after"].wait_recv()
             copies["on"].start()
             copies["partner_before"].start()
@@ -154,48 +153,64 @@
             copies["back"].start()
             copies["partner_after"].start()
         if 2 <= number:
-            copies, _ = made[number - 2]
+            copies = made[number - 2]
             copies["on"].wait_recv()
             copies["partner_left"].start()
             copies["back"].wait_recv()
             copies["partner_right"].start()
-    for copies, local in made:
+    for copies in made:
         for kind in ("partner", "partner_before", "partner_after", "partner_left", "partner_right"):
             copies[kind].wait_recv()
         for one in copies.values():
             one.wait_send()
-        for one in local:
-            one.wait()
     for one in part_copies:
         one.wait_send()
 
 
+def store_kernel(*refs):
+    *refs, sem = refs
+    some = len(refs) // 2
+    copies = [pltpu.make_async_copy(refs[k], refs[some + k], sem.at[k]) for k in range(some)]
+    for one in copies:
+        one.start()
+    for one in copies:
+        one.wait()
+
+
 def finish(n, gradients, weights, m, v):
     count = float(sum(w.size for w in weights))
+    layers = len(gradients[0])
     pieces = []
     for i in (2, 0, 1):
-        layers, rows, _ = gradients[i].shape
+        rows, _ = gradients[i][0].shape
         for layer in range(layers):
             for half in range(2):
                 pieces.append((i, layer, half * rows // 2, rows // 2))
-    anywhere = pl.BlockSpec(memory_space=pl.ANY)
-    shapes = [t.shape for t in gradients]
-    of = lambda dtype: [pltpu.VMEM(s, dtype) for s in shapes]
+    anywhere, inside = pl.BlockSpec(memory_space=pl.ANY), pl.BlockSpec(memory_space=pltpu.VMEM)
     dma = pltpu.SemaphoreType.DMA
+    results = [*weights, *m, *v]
+    ready = pl.pallas_call(
+        functools.partial(finish_kernel, n, count, tuple(pieces)),
+        out_shape=[pltpu.VMEM(t.shape, t.dtype) for t in results],
+        in_specs=[anywhere] * (3 * layers + 9),
+        out_specs=[inside] * 9,
+        scratch_shapes=[
+            *[pltpu.VMEM((layers, *one[0].shape), BF16) for one in gradients],
+            pltpu.VMEM((n, 8, 128), F32),
+            dma((3 * layers + 9,)), dma((n - 1,)), dma((n - 1,)), dma((9, len(pieces))), dma((9, len(pieces))),
+        ],
+        compiler_params=pltpu.CompilerParams(collective_id=4, has_side_effects=True, vmem_limit_bytes=7 * 2**20),
+        name="finish",
+    )(*sum(gradients, ()), *weights, *m, *v)
     return pl.pallas_call(
-        functools.partial(finish_kernel, n, count, tuple(pieces)),
-        out_shape=[jax.ShapeDtypeStruct(t.shape, t.dtype) for t in (*weights, *m, *v)],
-        in_specs=[anywhere] * 12,
+        store_kernel,
+        out_shape=[jax.ShapeDtypeStruct(t.shape, t.dtype) for t in results],
+        in_specs=[inside] * 9,
         out_specs=[anywhere] * 9,
-        scratch_shapes=[
-            *of(BF16), *of(BF16), *of(F32), *of(F32), *of(BF16),
-            pltpu.VMEM((n, 8, 128), F32),
-            dma((12,)), dma((len(pieces),)), dma((2, len(pieces))), dma((n - 1,)), dma((n - 1,)),
-            dma((9, len(pieces))), dma((9, len(pieces))),
-        ],
-        compiler_params=pltpu.CompilerParams(collective_id=4, has_side_effects=True, vmem_limit_bytes=48 * 2**20),
-        name="finish",
-    )(*gradients, *weights, *m, *v)
+        scratch_shapes=[dma((9,))],
+        compiler_params=pltpu.CompilerParams(vmem_limit_bytes=7*2**20),
+        name="store",
+    )(*[pltpu.with_memory_space_constraint(t, pltpu.VMEM) for t in ready])
 
 
 def dot(a, b, contract=((1,), (0,))):
@@ -286,13 +301,12 @@
     )(x, w_gate, w_up, w_down)
 
 
-SLOTS = 6
-HELD = 4
 SENT = 3
 
 
 class Exchange:
-    def __init__(self, n, refs, kinds):
+    def __init__(self, n, refs, kinds, lags):
+        self.lags = lags
         self.mine, self.pair, self.out2, self.out3, self.in2, self.in3, self.pair_sem, self.sem2, self.sem3 = refs
         self.kinds = kinds
         self.me, self.core, self.partner, self.after, self.before, _ = places("dp", n)
@@ -302,17 +316,24 @@
         self.chip_after, self.chip_before, self.chip_across = (lax.rem(chip + k, chips) for k in (1, chips - 1, chips // 2))
 
     @staticmethod
-    def scratch(n, rows, width):
+    def scratch(n, rows, width, lags):
         chips, half, dma = n // CORES, width // 2, pltpu.SemaphoreType.DMA
+        held, slots = lags[3] + 1, lags[3] + 3
         return [
-            pltpu.VMEM((HELD, chips, CORES, rows, width), BF16),
-            pltpu.VMEM((SLOTS, chips, rows, width), BF16),
+            pltpu.VMEM((held, chips, CORES, rows, width), BF16),
+            pltpu.VMEM((slots, chips, rows, width), BF16),
             pltpu.VMEM((2, SENT, rows, width), BF16),
             pltpu.VMEM((2, SENT, rows, half), BF16),
-            pltpu.VMEM((2, SLOTS, rows, width), BF16),
-            pltpu.VMEM((2, SLOTS, rows, half), BF16),
-            dma((2, SLOTS)), dma((2, 2, SLOTS)), dma((2, 2, SLOTS)),
+            pltpu.VMEM((2, slots, rows, width), BF16),
+            pltpu.VMEM((2, slots, rows, half), BF16),
+            dma((2, slots)), dma((2, 2, slots)), dma((2, 2, slots)),
         ]
+
+    def slot(self, p):
+        return lax.rem(p, self.pair.shape[0])
+
+    def held(self, p):
+        return lax.rem(p, self.mine.shape[0])
 
     def barrier(self):
         barrier = pltpu.get_barrier_semaphore()
@@ -321,14 +342,14 @@
         pl.semaphore_wait(barrier, 3)
 
     def copy1(self, p, rows):
-        slot = lax.rem(p, SLOTS)
+        slot = self.slot(p)
         return pltpu.make_async_remote_copy(
-            self.mine.at[lax.rem(p, HELD), :, 1 - self.core, pl.ds(0, rows)], self.pair.at[slot, :, pl.ds(0, rows)],
+            self.mine.at[self.held(p), :, 1 - self.core, pl.ds(0, rows)], self.pair.at[slot, :, pl.ds(0, rows)],
             self.pair_sem.at[0, slot], self.pair_sem.at[1, slot], device_id={"dp": self.partner}, device_id_type=MESH,
         )
 
     def copies(self, p, rows, out, into, sem):
-        slot = lax.rem(p, SLOTS)
+        slot = self.slot(p)
         return [
             pltpu.make_async_remote_copy(
                 out.at[way, lax.rem(p, SENT), pl.ds(0, rows)], into.at[way, slot, pl.ds(0, rows)],
@@ -338,15 +359,11 @@
         ]
 
     def over(self, rows, body):
-        def step(i, _):
-            body(pl.ds(pl.multiple_of(i * 16, 16), 16))
-            return 0
-
-        lax.fori_loop(0, rows // 16, step, 0)
+        body(pl.ds(0, rows))
 
     def of_chip(self, p, chip, at, columns):
-        a = self.mine[lax.rem(p, HELD), chip, self.core, at, columns].astype(F32)
-        return a + self.pair[lax.rem(p, SLOTS), chip, at, columns].astype(F32)
+        a = self.mine[self.held(p), chip, self.core, at, columns].astype(F32)
+        return a + self.pair[self.slot(p), chip, at, columns].astype(F32)
 
     def stage1(self, p, rows, _):
         self.copy1(p, rows).start()
@@ -370,7 +387,7 @@
     def stage3(self, p, rows, _):
         for one in self.copies(p, rows, self.out2, self.in2, self.sem2):
             one.wait()
-        slot, arrived = lax.rem(p, SENT), lax.rem(p, SLOTS)
+        slot, arrived = lax.rem(p, SENT), self.slot(p)
         half = self.out3.shape[-1]
         left, right = slice(0, half), slice(half, 2 * half)
 
@@ -385,7 +402,7 @@
     def stage4(self, p, rows, keep):
         for one in self.copies(p, rows, self.out3, self.in3, self.sem3):
             one.wait()
-        arrived = lax.rem(p, SLOTS)
+        arrived = self.slot(p)
         half = self.out3.shape[-1]
         left, right = slice(0, half), slice(half, 2 * half)
 
@@ -397,7 +414,7 @@
         self.over(rows, body)
 
     def move(self, step, low, high):
-        for lag, stage in enumerate((self.stage1, self.stage2, self.stage3, self.stage4)):
+        for lag, stage in zip(self.lags, (self.stage1, self.stage2, self.stage3, self.stage4), strict=True):
             for first, end, rows, keep in self.kinds:
                 if high - 1 - lag < first or low - lag >= end:
                     continue
@@ -436,9 +453,10 @@
     start = pl.multiple_of(lax.rem(which, 2) * rows, 16)
     columns = pl.ds(pl.multiple_of(lax.div(which, 2) * width, width), width)
     share = n_rows // (chips * cores)
-    lhs = jnp.concatenate([hidden_t[pl.ds(pl.multiple_of(k * share + start, 16), rows), :] for k in range(chips * cores)], 0)
-    block = dot(lhs, by_out[:, columns]).astype(BF16)
-    exchange.mine[lax.rem(step, HELD)] = block.reshape(chips, cores, rows, width)
+    by_out = by_out[:, columns]
+    for k in range(chips * cores):
+        lhs = hidden_t[pl.ds(pl.multiple_of(k * share + start, 16), rows), :]
+        exchange.mine[exchange.held(step), k // cores, k % cores] = dot(lhs, by_out).astype(BF16)
 
 
 def wide_packet(exchange, step, a_t, by_both):
@@ -448,10 +466,12 @@
     for k in range(2):
         columns = slice(k * half, k * half + half)
         block = dot(a_t[...], by_both[:, columns]).astype(BF16)
-        exchange.mine[lax.rem(step, HELD), :, :, pl.ds(0, rows), columns] = block.reshape(chips, cores, rows, half)
+        exchange.mine[exchange.held(step), :, :, pl.ds(0, rows), columns] = block.reshape(chips, cores, rows, half)
 
 
 MB = 512
+TOP_LAGS = (0, 1, 2, 3)
+BOTTOM_LAGS = (0, 1, 3, 5)
 
 
 def top_kernel(n, *refs):
@@ -470,6 +490,7 @@
             (0, chunks, wide_rows, keep_columns(0, g_gate, g_up, width)),
             (chunks, chunks + downs, down_rows, keep_down(chunks, g_down, down_rows, 2 * width)),
         ),
+        TOP_LAGS,
     )
     layer = w_gate.shape[0] - 1
     first, rest = pl.ds(0, width), pl.ds(width, ff - width)
@@ -567,15 +588,14 @@
     for one in tile_loads(0):
         one.start()
 
-    def down(step, _):
-        down_packet(exchange, step, chunks, hidden_t, dy)
-        exchange.move(step, chunks, chunks + downs)
-        return 0
-
-    lax.fori_loop(chunks, chunks + downs, down, 0)
-
     def tile(step, _):
-        t = step - chunks - downs
+        t = step - chunks
+
+        @pl.when(t < downs)
+        def _():
+            down_packet(exchange, step, chunks, hidden_t, dy)
+
+        exchange.move(step, chunks, chunks + tiles)
         slot = lax.rem(t, 2)
         for one in tile_loads(t):
             one.wait()
@@ -597,10 +617,9 @@
         rows = pl.ds(pl.multiple_of(t * tile_rows, tile_rows), tile_rows)
         by_tile[slot] = (dy[rows].astype(F32) + by_norm(h_tile[slot], total)).astype(BF16)
         tile_store(t).start()
-        exchange.move(step, chunks + downs, chunks + downs + tiles)
         return 0
 
-    lax.fori_loop(chunks + downs, chunks + downs + tiles, tile, 0)
+    lax.fori_loop(chunks, chunks + tiles, tile, 0)
     for t in (tiles - 2, tiles - 1):
         tile_store(t).wait()
 
@@ -629,7 +648,7 @@
             pltpu.VMEM((2, width, d), BF16), pltpu.VMEM((2, tokens, 2 * width), BF16),
             pltpu.VMEM((2, 256, d), BF16), pltpu.VMEM((2, 256, d), BF16),
             dma((7,)), dma((2,)), dma((2, 2)), dma((5, 2)), dma((2,)),
-            *Exchange.scratch(n, ff // n // 2, 2 * width),
+            *Exchange.scratch(n, ff // n // 2, 2 * width, TOP_LAGS),
         ],
         compiler_params=pltpu.CompilerParams(collective_id=2, has_side_effects=True, vmem_limit_bytes=67043328),
         name="top",
@@ -652,12 +671,17 @@
             (0, downs, down_rows, keep_down(0, g_down, down_rows, 2 * width)),
             (downs, downs + chunks, wide_rows, keep_columns(downs, g_gate, g_up, width)),
         ),
+        BOTTOM_LAGS,
     )
-    loads = [
-        pltpu.make_async_copy(ht_in, hidden_t, load_sem.at[0]),
-        pltpu.make_async_copy(by_in, by, load_sem.at[1]),
-        pltpu.make_async_copy(at_in, a_t, load_sem.at[2]),
-    ]
+    share = ff // n
+    halves = lambda ref, k: ref.at[:, pl.ds(k * 2 * width, 2 * width)]
+    loads = [pltpu.make_async_copy(halves(by_in, 0), halves(by, 0), load_sem.at[0])]
+    for k in range(2):
+        for to in range(n):
+            rows = pl.ds(to * share + k * down_rows, down_rows)
+            loads.append(pltpu.make_async_copy(ht_in.at[rows], hidden_t.at[rows], load_sem.at[3 + k * n + to]))
+    loads.append(pltpu.make_async_copy(halves(by_in, 1), halves(by, 1), load_sem.at[1]))
+    loads.append(pltpu.make_async_copy(at_in, a_t, load_sem.at[2]))
 
     def chunk_loads(c):
         slot = lax.rem(c, 2)
@@ -671,16 +695,23 @@
     for one in (*loads, *chunk_loads(0)):
         one.start()
     exchange.barrier()
-    for one in loads[:2]:
-        one.wait()
 
     def down(step, _):
+        @pl.when(step == 0)
+        def _():
+            for one in loads[: 1 + n]:
+                one.wait()
+
+        @pl.when(step == 1)
+        def _():
+            for one in loads[1 + n :]:
+                one.wait()
+
         down_packet(exchange, step, 0, hidden_t, by)
         exchange.move(step, 0, downs)
         return 0
 
     lax.fori_loop(0, downs, down, 0)
-    loads[2].wait()
 
     def chunk(step, _):
         c = step - downs
@@ -704,7 +735,7 @@
         return 0
 
     lax.fori_loop(downs, downs + chunks, chunk, 0)
-    for step in range(downs + chunks, downs + chunks + 3):
+    for step in range(downs + chunks, downs + chunks + BOTTOM_LAGS[-1]):
         exchange.move(step, step, step + 1)
 
 
@@ -727,8 +758,8 @@
             pltpu.VMEM((tokens, d), BF16), pltpu.VMEM((ff, tokens), BF16), pltpu.VMEM((d, tokens), BF16),
             pltpu.VMEM((2, width, d), BF16), pltpu.VMEM((2, tokens, width), F32), pltpu.VMEM((2, tokens, width), F32),
             pltpu.VMEM((tokens, 2 * width), BF16),
-            dma((3,)), dma((2,)), dma((2, 2)),
-            *Exchange.scratch(n, ff // n // 2, 2 * width),
+            dma((3 + 2 * n,)), dma((2,)), dma((2, 2)),
+            *Exchange.scratch(n, ff // n // 2, 2 * width, BOTTOM_LAGS),
         ],
         compiler_params=pltpu.CompilerParams(collective_id=3, has_side_effects=True, vmem_limit_bytes=67043328),
         name="bottom",
@@ -742,7 +773,7 @@
         gate, up, hidden_t, a_t, h, next_a, next_a_t = layer_0(x[0], w_gate, w_up, w_down)
         *top, by_h, _, _ = top_layer(n, next_a, next_a_t, h, dy[0], w_gate, w_up, w_down)
         bottom = bottom_layer(n, by_h, hidden_t, a_t, gate, up, w_down)
-        gradients = [jnp.stack(pair) for pair in zip(bottom, top, strict=True)]
+        gradients = list(zip(bottom, top, strict=True))
         return tuple(finish(n, gradients, (w_gate, w_up, w_down), moments[:3], moments[3:]))
 
     sharded = P(None, "dp", None)

time: 481 us -> 438 us (0.911)
  local copies, waits for them, and re-layouts: 40.3 us -> 0 us
    unnamed x33 -> x0, local copies, waits for them, and re-layouts: 40.3 us -> none
    pallas_call x0 -> x1, Pallas kernels: none -> 16.7 us  [finish(): pl.pallas_call(store_kernel, out_shape=[jax.ShapeDtypeStruct(t.shape, t.d...]
    pallas_call x1, Pallas kernels: 95.4 us -> 86.1 us  [bottom_layer(): pl.pallas_call(functools.partial(bottom_kernel, n), in_specs=[anywhere] *...]
    pallas_call x1, Pallas kernels: 134 us -> 127 us  [top_layer(): pl.pallas_call(functools.partial(top_kernel, n), in_specs=[anywhere] * 7,...]
where the time goes in v1:
time: 438 us
  Pallas kernels  437 us (100%)
    pallas_call x1, Pallas kernels, finish(): pl.pallas_call(functools.partial(finish_kernel, n, count, tuple(pieces)),...  155 us
    pallas_call x1, Pallas kernels, top_layer(): pl.pallas_call(functools.partial(top_kernel, n), in_specs=[anywhere] * 7,...  127 us
    pallas_call x1, Pallas kernels, bottom_layer(): pl.pallas_call(functools.partial(bottom_kernel, n), in_specs=[anywhere] *...  86.1 us
    pallas_call x1, Pallas kernels, layer_0(): pl.pallas_call(functools.partial(forward_kernel, tokens // rows), grid=(t...  52 us
    pallas_call x1, Pallas kernels, finish(): pl.pallas_call(store_kernel, out_shape=[jax.ShapeDtypeStruct(t.shape, t.d...  16.7 us

profile of v1, /device:TPU:113, one launch (start us, length us, event | category | flops | bytes accessed | tf_op | source)
XLA Modules:
  0.0 437.6 jit_solution(7041460768987216209)
XLA Ops:
  0.6 52.0 %forward.1 = (f32[2048,2816]{1,0:T(8,128)}, f32[2048,2816]{1,0:T(8,128)}, bf16[2816,2048]{1,0:T(8,128)(2,1)}, bf16[1024,2048]{1,0:T(8,128)(2,1)}, bf16[2048,1024...) custom-call(bf16[2048,1024]{1,0:T(8,128)(2,1)} %bitcast.2, bf16[2,1024,2816]{2,1,0:T(8,128)(2,1)} %refs_6_.3, ...), custom_call_target="tpu_custom_call" | custom-call | tf_op jit(solution)/shard_map/forward/pallas_call | solution.py:284
  52.7 127.2 %top.1 = (bf16[128,2816]{1,0:T(8,128)(2,1)}, bf16[128,2816]{1,0:T(8,128)(2,1)}, bf16[352,1024]{1,0:T(8,128)(2,1)}, bf16[2048,1024]{1,0:T(8,128)(2,1)}, bf16[2048...) custom-call(bf16[2048,1024]{1,0:T(8,128)(2,1)} %get-tuple-element.32.refs_0_, ...), custom_call_target="tpu_custom_call" | custom-call | tf_op jit(solution)/shard_map/top/pallas_call | solution.py:633
  179.9 86.1 %bottom.1 = (bf16[128,2816]{1,0:T(8,128)(2,1)}, bf16[128,2816]{1,0:T(8,128)(2,1)}, bf16[352,1024]{1,0:T(8,128)(2,1)}) custom-call(bf16[2048,1024]{1,0:T(8,128)(2,1)} %get-tuple-element.35.refs_0_, bf16[2816,2048]{1,0:T(8,128)(2,1)} %get-tuple-element.36.refs_1_, bf16[1024,2048]{1,0:T(8,128)(2,1)} %get-tuple-element.37.refs_2_, ...), custom_call_target="tpu_custom_call" | custom-call | tf_op jit(solution)/shard_map/bottom/pallas_call | solution.py:748
  266.0 154.6 %finish.1 = (bf16[2,1024,2816]{2,1,0:T(8,128)(2,1)S(1)}, bf16[2,1024,2816]{2,1,0:T(8,128)(2,1)S(1)}, bf16[2,2816,1024]{2,1,0:T(8,128)(2,1)S(1)}, f32[2,128,2816]...) custom-call(bf16[128,2816]{1,0:T(8,128)(2,1)} %get-tuple-element.40., ...), custom_call_target="tpu_custom_call" | custom-call | tf_op jit(solution)/shard_map/finish/pallas_call | solution.py:192
  420.6 16.7 %store.1 = (bf16[2,1024,2816]{2,1,0:T(8,128)(2,1)}, bf16[2,1024,2816]{2,1,0:T(8,128)(2,1)}, bf16[2,2816,1024]{2,1,0:T(8,128)(2,1)}, f32[2,128,2816]{2,1,0:T(8,12...) custom-call(bf16[2,1024,2816]{2,1,0:T(8,128)(2,1)S(1)} %get-tuple-el, ...), custom_call_target="tpu_custom_call" | custom-call | tf_op jit(solution)/shard_map/store/pallas_call | solution.py:205

commit v2 on v1

--- a/solution.py
+++ b/solution.py
@@ -22,6 +22,7 @@
 
 def finish_kernel(n, count, pieces, *refs):
     layers = 2
+    squares, refs = refs[:layers], refs[layers:]
     g_in, refs = [refs[layers * i : layers * i + layers] for i in range(3)], refs[3 * layers :]
     w_in, m_in, v_in, w, m, v = (refs[3 * i : 3 * i + 3] for i in range(6))
     g, refs = refs[18:21], refs[21:]
@@ -37,35 +38,16 @@
         return pl.ds(pl.multiple_of(owner * g[i].shape[1] + first, 16), rows)
 
     order = (2, 0, 1)
-    g_loads = [[pltpu.make_async_copy(g_in[i][k], g[i].at[k], load_sem.at[layers * i + k]) for k in range(layers)] for i in order]
     loads = {}
-    at = 3 * layers
     for i in order:
         rows = rows_of(i, me, 0, g[i].shape[1])
-        loads[i] = [
-            pltpu.make_async_copy(w_in[i].at[:, rows], w[i].at[:, rows], load_sem.at[at]),
-            pltpu.make_async_copy(m_in[i], m[i], load_sem.at[at + 1]),
-            pltpu.make_async_copy(v_in[i], v[i], load_sem.at[at + 2]),
-        ]
-        at += 3
-    for one in (*sum(g_loads, []), *sum((loads[i] for i in order), [])):
+        pairs = [(w_in[i].at[:, rows], w[i].at[:, rows]), (m_in[i], m[i]), (v_in[i], v[i])]
+        pairs += [(g_in[i][k], g[i].at[k]) for k in range(layers)]
+        loads[i] = [pltpu.make_async_copy(src, dst, load_sem.at[i, k]) for k, (src, dst) in enumerate(pairs)]
+    for one in loads[order[0]]:
         one.start()
 
-    total = jnp.zeros((8, 128), F32)
-    for i, its_loads in zip(order, g_loads, strict=True):
-        _, rows, columns = g[i].shape
-        for one in its_loads:
-            one.wait()
-
-        def squares(step, total, ref=g[i], columns=columns, rows=rows):
-            block = ref[lax.div(step, rows // 16), pl.ds(pl.multiple_of(lax.rem(step, rows // 16) * 16, 16), 16), :].astype(F32)
-            block = block * block
-            sums = [block[:8, at : at + 128] + block[8:, at : at + 128] for at in range(0, columns, 128)]
-            while len(sums) > 1:
-                sums = [a + b for a, b in zip(sums[::2], sums[1::2])] + ([sums[-1]] if len(sums) % 2 else [])
-            return total + sums[0]
-
-        total = lax.fori_loop(0, layers * rows // 16, squares, total)
+    total = squares[0][...] + squares[1][...]
     parts[pl.ds(me, 1)] = total[None]
     pl.semaphore_wait(barrier, n - 1)
     part_copies = []
@@ -137,13 +119,18 @@
                 one.wait()
         adamw(i, layer, first, rows)
 
-    compute(0)
+    def own_piece(number):
+        compute(number)
+        for kind in ("after", "before", "partner"):
+            made[number][kind].start()
+
+    own_piece(0)
+    for i in order[1:]:
+        for one in loads[i]:
+            one.start()
     for number in range(total_pieces + 2):
         if number + 1 < total_pieces:
-            compute(number + 1)
-        if number < total_pieces:
-            for kind in ("after", "before", "partner"):
-                made[number][kind].start()
+            own_piece(number + 1)
         if 1 <= number <= total_pieces:
             copies = made[number - 1]
             copies["after"].wait_recv()
@@ -177,31 +164,37 @@
         one.wait()
 
 
-def finish(n, gradients, weights, m, v):
+def finish(n, gradients, squares, weights, m, v):
     count = float(sum(w.size for w in weights))
     layers = len(gradients[0])
     pieces = []
     for i in (2, 0, 1):
         rows, _ = gradients[i][0].shape
         for layer in range(layers):
-            for half in range(2):
-                pieces.append((i, layer, half * rows // 2, rows // 2))
+            half = rows // 2
+            cuts = [half, half]
+            if (i, layer) == (2, 0):
+                cuts = [48, half - 48, half]
+            elif (i, layer) == (1, layers - 1):
+                cuts = [half, half // 2, half // 4, half // 4]
+            for cut in cuts:
+                pieces.append((i, layer, sum(p[3] for p in pieces if p[:2] == (i, layer)), cut))
     anywhere, inside = pl.BlockSpec(memory_space=pl.ANY), pl.BlockSpec(memory_space=pltpu.VMEM)
     dma = pltpu.SemaphoreType.DMA
     results = [*weights, *m, *v]
     ready = pl.pallas_call(
         functools.partial(finish_kernel, n, count, tuple(pieces)),
         out_shape=[pltpu.VMEM(t.shape, t.dtype) for t in results],
-        in_specs=[anywhere] * (3 * layers + 9),
+        in_specs=[inside] * layers + [anywhere] * (3 * layers + 9),
         out_specs=[inside] * 9,
         scratch_shapes=[
             *[pltpu.VMEM((layers, *one[0].shape), BF16) for one in gradients],
             pltpu.VMEM((n, 8, 128), F32),
-            dma((3 * layers + 9,)), dma((n - 1,)), dma((n - 1,)), dma((9, len(pieces))), dma((9, len(pieces))),
+            dma((3, layers + 3)), dma((n - 1,)), dma((n - 1,)), dma((9, len(pieces))), dma((9, len(pieces))),
         ],
         compiler_params=pltpu.CompilerParams(collective_id=4, has_side_effects=True, vmem_limit_bytes=7 * 2**20),
         name="finish",
-    )(*sum(gradients, ()), *weights, *m, *v)
+    )(*squares, *sum(gradients, ()), *weights, *m, *v)
     return pl.pallas_call(
         store_kernel,
         out_shape=[jax.ShapeDtypeStruct(t.shape, t.dtype) for t in results],
@@ -241,7 +234,7 @@
 
     @pl.when(tile == 0)
     def _():
-        for one in loads:
+        for one in loads[:2]:
             one.start()
 
     a = normed(x[...])
@@ -251,6 +244,7 @@
     def _():
         loads[0].wait()
         loads[1].wait()
+        loads[2].start()
 
     columns = wg.shape[1]
     width = 256
@@ -301,36 +295,34 @@
     )(x, w_gate, w_up, w_down)
 
 
-SENT = 3
-
-
 class Exchange:
     def __init__(self, n, refs, kinds, lags):
+        self.mine, self.pair, self.out2, self.out3, self.in2, self.in3, self.own, self.side, self.pair_sem, self.sem2, self.sem3 = refs
+        self.kinds = kinds
         self.lags = lags
-        self.mine, self.pair, self.out2, self.out3, self.in2, self.in3, self.pair_sem, self.sem2, self.sem3 = refs
-        self.kinds = kinds
         self.me, self.core, self.partner, self.after, self.before, _ = places("dp", n)
         chips = n // CORES
-        chip = lax.div(self.me, CORES)
-        self.chip = chip
-        self.chip_after, self.chip_before, self.chip_across = (lax.rem(chip + k, chips) for k in (1, chips - 1, chips // 2))
+        self.chip = lax.div(self.me, CORES)
+        self.chip_after, self.chip_before, self.chip_across = (lax.rem(self.chip + k, chips) for k in (1, chips - 1, chips // 2))
+        half = self.out3.shape[-1]
+        self.left, self.right = slice(0, half), slice(half, 2 * half)
 
     @staticmethod
     def scratch(n, rows, width, lags):
         chips, half, dma = n // CORES, width // 2, pltpu.SemaphoreType.DMA
-        held, slots = lags[3] + 1, lags[3] + 3
+        _, two, three, four = lags
+        slots1, slots2, slots3 = two + 3, 2 * (three - two) + 2, 2 * (four - three) + 2
         return [
-            pltpu.VMEM((held, chips, CORES, rows, width), BF16),
-            pltpu.VMEM((slots, chips, rows, width), BF16),
-            pltpu.VMEM((2, SENT, rows, width), BF16),
-            pltpu.VMEM((2, SENT, rows, half), BF16),
-            pltpu.VMEM((2, slots, rows, width), BF16),
-            pltpu.VMEM((2, slots, rows, half), BF16),
-            dma((2, slots)), dma((2, 2, slots)), dma((2, 2, slots)),
+            pltpu.VMEM((two + 1, chips, CORES, rows, width), BF16),
+            pltpu.VMEM((slots1, chips, rows, width), BF16),
+            pltpu.VMEM((2, three - two + 1, rows, width), BF16),
+            pltpu.VMEM((2, four - three + 1, rows, half), BF16),
+            pltpu.VMEM((2, slots2, rows, width), BF16),
+            pltpu.VMEM((2, slots3, rows, half), BF16),
+            pltpu.VMEM((four - two + 1, rows, width), F32),
+            pltpu.VMEM((2, three - two + 1, rows, half), F32),
+            dma((2, slots1)), dma((2, 2, slots2)), dma((2, 2, slots3)),
         ]
-
-    def slot(self, p):
-        return lax.rem(p, self.pair.shape[0])
 
     def held(self, p):
         return lax.rem(p, self.mine.shape[0])
@@ -342,76 +334,71 @@
         pl.semaphore_wait(barrier, 3)
 
     def copy1(self, p, rows):
-        slot = self.slot(p)
+        slot = lax.rem(p, self.pair.shape[0])
         return pltpu.make_async_remote_copy(
             self.mine.at[self.held(p), :, 1 - self.core, pl.ds(0, rows)], self.pair.at[slot, :, pl.ds(0, rows)],
             self.pair_sem.at[0, slot], self.pair_sem.at[1, slot], device_id={"dp": self.partner}, device_id_type=MESH,
         )
 
     def copies(self, p, rows, out, into, sem):
-        slot = self.slot(p)
+        slot = lax.rem(p, into.shape[1])
         return [
             pltpu.make_async_remote_copy(
-                out.at[way, lax.rem(p, SENT), pl.ds(0, rows)], into.at[way, slot, pl.ds(0, rows)],
+                out.at[way, lax.rem(p, out.shape[1]), pl.ds(0, rows)], into.at[way, slot, pl.ds(0, rows)],
                 sem.at[0, way, slot], sem.at[1, way, slot], device_id={"dp": to}, device_id_type=MESH,
             )
             for way, to in enumerate((self.after, self.before))
         ]
 
-    def over(self, rows, body):
-        body(pl.ds(0, rows))
-
-    def of_chip(self, p, chip, at, columns):
-        a = self.mine[self.held(p), chip, self.core, at, columns].astype(F32)
-        return a + self.pair[self.slot(p), chip, at, columns].astype(F32)
+    def copies2(self, p, rows):
+        return self.copies(p, rows, self.out2, self.in2, self.sem2)
+
+    def copies3(self, p, rows):
+        return self.copies(p, rows, self.out3, self.in3, self.sem3)
 
     def stage1(self, p, rows, _):
         self.copy1(p, rows).start()
 
     def stage2(self, p, rows, _):
         self.copy1(p, rows).wait()
-        slot = lax.rem(p, SENT)
-        half = self.out3.shape[-1]
-        left, right = slice(0, half), slice(half, 2 * half)
-
-        def body(at):
-            self.out2[0, slot, at, left] = self.of_chip(p, self.chip_across, at, left).astype(BF16)
-            self.out2[0, slot, at, right] = self.of_chip(p, self.chip_after, at, right).astype(BF16)
-            self.out2[1, slot, at, left] = self.of_chip(p, self.chip_before, at, left).astype(BF16)
-            self.out2[1, slot, at, right] = self.of_chip(p, self.chip_across, at, right).astype(BF16)
-
-        self.over(rows, body)
-        for one in self.copies(p, rows, self.out2, self.in2, self.sem2):
+        slot, own, side = (lax.rem(p, t.shape[k]) for t, k in ((self.out2, 1), (self.own, 0), (self.side, 1)))
+        at = slice(0, rows)
+
+        def of_chip(chip, columns):
+            a = self.mine[self.held(p), chip, self.core, at, columns].astype(F32)
+            return a + self.pair[lax.rem(p, self.pair.shape[0]), chip, at, columns].astype(F32)
+
+        self.out2[0, slot, at, self.left] = of_chip(self.chip_across, self.left).astype(BF16)
+        self.out2[0, slot, at, self.right] = of_chip(self.chip_after, self.right).astype(BF16)
+        self.out2[1, slot, at, self.left] = of_chip(self.chip_before, self.left).astype(BF16)
+        self.out2[1, slot, at, self.right] = of_chip(self.chip_across, self.right).astype(BF16)
+        for one in self.copies2(p, rows):
             one.start()
+        self.side[0, side, at] = of_chip(self.chip_after, self.left)
+        self.side[1, side, at] = of_chip(self.chip_before, self.right)
+        for columns in (self.left, self.right):
+            self.own[own, at, columns] = of_chip(self.chip, columns)
 
     def stage3(self, p, rows, _):
-        for one in self.copies(p, rows, self.out2, self.in2, self.sem2):
+        for one in self.copies2(p, rows):
             one.wait()
-        slot, arrived = lax.rem(p, SENT), self.slot(p)
-        half = self.out3.shape[-1]
-        left, right = slice(0, half), slice(half, 2 * half)
-
-        def body(at):
-            self.out3[0, slot, at] = (self.of_chip(p, self.chip_after, at, left) + self.in2[0, arrived, at, left].astype(F32)).astype(BF16)
-            self.out3[1, slot, at] = (self.of_chip(p, self.chip_before, at, right) + self.in2[1, arrived, at, right].astype(F32)).astype(BF16)
-
-        self.over(rows, body)
-        for one in self.copies(p, rows, self.out3, self.in3, self.sem3):
+        slot, arrived, own, side = (lax.rem(p, t.shape[k]) for t, k in ((self.out3, 1), (self.in2, 1), (self.own, 0), (self.side, 1)))
+        at = slice(0, rows)
+        self.out3[0, slot, at] = (self.side[0, side, at] + self.in2[0, arrived, at, self.left].astype(F32)).astype(BF16)
+        self.out3[1, slot, at] = (self.side[1, side, at] + self.in2[1, arrived, at, self.right].astype(F32)).astype(BF16)
+        for one in self.copies3(p, rows):
             one.start()
+        self.own[own, at, self.left] += self.in2[1, arrived, at, self.left].astype(F32)
+        self.own[own, at, self.right] += self.in2[0, arrived, at, self.right].astype(F32)
 
     def stage4(self, p, rows, keep):
-        for one in self.copies(p, rows, self.out3, self.in3, self.sem3):
+        for one in self.copies3(p, rows):
             one.wait()
-        arrived = self.slot(p)
-        half = self.out3.shape[-1]
-        left, right = slice(0, half), slice(half, 2 * half)
-
-        def body(at):
-            a = self.of_chip(p, self.chip, at, left) + (self.in3[0, arrived, at].astype(F32) + self.in2[1, arrived, at, left].astype(F32))
-            b = self.of_chip(p, self.chip, at, right) + (self.in2[0, arrived, at, right].astype(F32) + self.in3[1, arrived, at].astype(F32))
-            keep(p, at, a.astype(BF16), b.astype(BF16))
-
-        self.over(rows, body)
+        arrived, own = lax.rem(p, self.in3.shape[1]), lax.rem(p, self.own.shape[0])
+        at = slice(0, rows)
+        a = self.own[own, at, self.left] + self.in3[0, arrived, at].astype(F32)
+        b = self.own[own, at, self.right] + self.in3[1, arrived, at].astype(F32)
+        keep(p, a.astype(BF16), b.astype(BF16))
 
     def move(self, step, low, high):
         for lag, stage in zip(self.lags, (self.stage1, self.stage2, self.stage3, self.stage4), strict=True):
@@ -425,23 +412,36 @@
                     pl.when((p >= first) & (p < end))(functools.partial(stage, p, rows, keep))
 
 
-def keep_columns(first, gate, up, width):
-    def keep(p, at, left, right):
+def add_squares(total, *blocks):
+    for block in blocks:
+        wide = block.astype(F32)
+        wide = wide * wide
+        rows, columns = wide.shape
+        sums = [wide[r : r + 8, c : c + 128] for r in range(0, rows, 8) for c in range(0, columns, 128)]
+        while len(sums) > 1:
+            sums = [a + b for a, b in zip(sums[::2], sums[1::2])] + ([sums[-1]] if len(sums) % 2 else [])
+        total[...] += sums[0]
+
+
+def keep_columns(first, gate, up, width, squares):
+    def keep(p, left, right):
         columns = pl.ds(pl.multiple_of((p - first) * width, width), width)
-        gate[at, columns] = left
-        up[at, columns] = right
+        gate[:, columns] = left
+        up[:, columns] = right
+        add_squares(squares, left, right)
 
     return keep
 
 
-def keep_down(first, down, rows, width):
-    def keep(p, at, left, right):
+def keep_down(first, down, rows, width, squares):
+    def keep(p, left, right):
         half = width // 2
         which = p - first
-        at = pl.ds(pl.multiple_of(lax.rem(which, 2) * rows + at.start, 16), at.size)
+        at = pl.ds(pl.multiple_of(lax.rem(which, 2) * rows, 16), rows)
         start = lax.div(which, 2) * width
         down[at, pl.ds(pl.multiple_of(start, half), half)] = left
         down[at, pl.ds(pl.multiple_of(start + half, half), half)] = right
+        add_squares(squares, left, right)
 
     return keep
 
@@ -470,13 +470,13 @@
 
 
 MB = 512
-TOP_LAGS = (0, 1, 2, 3)
+TOP_LAGS = (0, 1, 3, 5)
 BOTTOM_LAGS = (0, 1, 3, 5)
 
 
 def top_kernel(n, *refs):
     (a_in, at_in, h_in, dy_in, w_gate, w_up, w_down), refs = refs[:7], refs[7:]
-    (g_gate, g_up, g_down, by_h, bg_hbm, bu_hbm), refs = refs[:6], refs[6:]
+    (g_gate, g_up, g_down, squares, by_h, bg_hbm, bu_hbm), refs = refs[:7], refs[7:]
     (a, a_t, dy, wg, wu, hidden_t, wd, both, h_tile, by_tile, load_sem, wd_sem, both_sem, tile_sem, by_sem), refs = refs[:15], refs[15:]
     tokens, d = a.shape
     ff = wg.shape[1]
@@ -487,8 +487,8 @@
     exchange = Exchange(
         n, refs,
         (
-            (0, chunks, wide_rows, keep_columns(0, g_gate, g_up, width)),
-            (chunks, chunks + downs, down_rows, keep_down(chunks, g_down, down_rows, 2 * width)),
+            (0, chunks, wide_rows, keep_columns(0, g_gate, g_up, width, squares)),
+            (chunks, chunks + downs, down_rows, keep_down(chunks, g_down, down_rows, 2 * width, squares)),
         ),
         TOP_LAGS,
     )
@@ -508,11 +508,10 @@
         slot = lax.rem(c, 2)
         return pltpu.make_async_copy(w_down.at[layer, pl.ds(pl.multiple_of(c * width, width), width)], wd.at[slot], wd_sem.at[slot])
 
-    for one in loads[:4]:
+    for one in loads[:5]:
         one.start()
     down_chunk(0).start()
-    for one in loads[4:]:
-        one.start()
+    squares[...] = jnp.zeros_like(squares)
     exchange.barrier()
 
     def store_both(c, k):
@@ -530,6 +529,8 @@
         def _():
             for one in loads[:5]:
                 one.wait()
+            for one in loads[5:]:
+                one.start()
 
         @pl.when(c == 1)
         def _():
@@ -620,6 +621,8 @@
         return 0
 
     lax.fori_loop(chunks, chunks + tiles, tile, 0)
+    for step in range(chunks + tiles, chunks + downs + TOP_LAGS[-1]):
+        exchange.move(step, step, step + 1)
     for t in (tiles - 2, tiles - 1):
         tile_store(t).wait()
 
@@ -633,11 +636,12 @@
     return pl.pallas_call(
         functools.partial(top_kernel, n),
         in_specs=[anywhere] * 7,
-        out_specs=[inside] * 3 + [anywhere] * 3,
+        out_specs=[inside] * 4 + [anywhere] * 3,
         out_shape=[
             jax.ShapeDtypeStruct((d // n, ff), BF16),
             jax.ShapeDtypeStruct((d // n, ff), BF16),
             jax.ShapeDtypeStruct((ff // n, d), BF16),
+            jax.ShapeDtypeStruct((8, 128), F32),
             jax.ShapeDtypeStruct((tokens, d), BF16),
             jax.ShapeDtypeStruct((tokens, ff), BF16),
             jax.ShapeDtypeStruct((tokens, ff), BF16),
@@ -657,7 +661,7 @@
 
 def bottom_kernel(n, *refs):
     (by_in, ht_in, at_in, gate_in, up_in, w_down), refs = refs[:6], refs[6:]
-    (g_gate, g_up, g_down), refs = refs[:3], refs[3:]
+    (g_gate, g_up, g_down, squares), refs = refs[:4], refs[4:]
     (by, hidden_t, a_t, wd, gate, up, both, load_sem, wd_sem, unit_sem), refs = refs[:10], refs[10:]
     tokens, d = by.shape
     ff = hidden_t.shape[0]
@@ -668,8 +672,8 @@
     exchange = Exchange(
         n, refs,
         (
-            (0, downs, down_rows, keep_down(0, g_down, down_rows, 2 * width)),
-            (downs, downs + chunks, wide_rows, keep_columns(downs, g_gate, g_up, width)),
+            (0, downs, down_rows, keep_down(0, g_down, down_rows, 2 * width, squares)),
+            (downs, downs + chunks, wide_rows, keep_columns(downs, g_gate, g_up, width, squares)),
         ),
         BOTTOM_LAGS,
     )
@@ -692,19 +696,30 @@
             pltpu.make_async_copy(up_in.at[:, columns], up.at[slot], unit_sem.at[1, slot]),
         ]
 
-    for one in (*loads, *chunk_loads(0)):
+    first, second, third = loads[: 1 + n], loads[1 + n : 1 + 2 * n], (*loads[1 + 2 * n :], *chunk_loads(0))
+    for one in first:
         one.start()
+    squares[...] = jnp.zeros_like(squares)
     exchange.barrier()
 
     def down(step, _):
         @pl.when(step == 0)
         def _():
-            for one in loads[: 1 + n]:
+            for one in first:
                 one.wait()
+            for one in second:
+                one.start()
 
         @pl.when(step == 1)
         def _():
-            for one in loads[1 + n :]:
+            for one in second:
+                one.wait()
+            for one in third:
+                one.start()
+
+        @pl.when(step == 2)
+        def _():
+            for one in third[:2]:
                 one.wait()
 
         down_packet(exchange, step, 0, hidden_t, by)
@@ -748,11 +763,12 @@
     return pl.pallas_call(
         functools.partial(bottom_kernel, n),
         in_specs=[anywhere] * 6,
-        out_specs=[inside] * 3,
+        out_specs=[inside] * 4,
         out_shape=[
             jax.ShapeDtypeStruct((d // n, ff), BF16),
             jax.ShapeDtypeStruct((d // n, ff), BF16),
             jax.ShapeDtypeStruct((ff // n, d), BF16),
+            jax.ShapeDtypeStruct((8, 128), F32),
         ],
         scratch_shapes=[
             pltpu.VMEM((tokens, d), BF16), pltpu.VMEM((ff, tokens), BF16), pltpu.VMEM((d, tokens), BF16),
@@ -771,10 +787,10 @@
 
     def step(x, dy, w_gate, w_up, w_down, *moments):
         gate, up, hidden_t, a_t, h, next_a, next_a_t = layer_0(x[0], w_gate, w_up, w_down)
-        *top, by_h, _, _ = top_layer(n, next_a, next_a_t, h, dy[0], w_gate, w_up, w_down)
-        bottom = bottom_layer(n, by_h, hidden_t, a_t, gate, up, w_down)
+        *top, squares_1, by_h, _, _ = top_layer(n, next_a, next_a_t, h, dy[0], w_gate, w_up, w_down)
+        *bottom, squares_0 = bottom_layer(n, by_h, hidden_t, a_t, gate, up, w_down)
         gradients = list(zip(bottom, top, strict=True))
-        return tuple(finish(n, gradients, (w_gate, w_up, w_down), moments[:3], moments[3:]))
+        return tuple(finish(n, gradients, (squares_0, squares_1), (w_gate, w_up, w_down), moments[:3], moments[3:]))
 
     sharded = P(None, "dp", None)
     return jax.shard_map(

time: 438 us -> 431 us (0.984)
  Pallas kernels: 437 us -> 430 us
    pallas_call x1, Pallas kernels: 127 us -> 122 us  [top_layer(): pl.pallas_call(functools.partial(top_kernel, n), in_specs=[anywhere] * 7,...]
where the time goes in v2:
time: 431 us
  Pallas kernels  430 us (100%)
    pallas_call x1, Pallas kernels, finish(): pl.pallas_call(functools.partial(finish_kernel, n, count, tuple(pieces)),...  156 us
    pallas_call x1, Pallas kernels, top_layer(): pl.pallas_call(functools.partial(top_kernel, n), in_specs=[anywhere] * 7,...  122 us
    pallas_call x1, Pallas kernels, bottom_layer(): pl.pallas_call(functools.partial(bottom_kernel, n), in_specs=[anywhere] *...  82.4 us
    pallas_call x1, Pallas kernels, layer_0(): pl.pallas_call(functools.partial(forward_kernel, tokens // rows), grid=(t...  52 us
    pallas_call x1, Pallas kernels, finish(): pl.pallas_call(store_kernel, out_shape=[jax.ShapeDtypeStruct(t.shape, t.d...  16.7 us

profile of v2, /device:TPU:113, one launch (start us, length us, event | category | flops | bytes accessed | tf_op | source)
XLA Modules:
  0.0 430.7 jit_solution(17560524502789767473)
XLA Ops:
  0.6 52.0 %forward.1 = (f32[2048,2816]{1,0:T(8,128)}, f32[2048,2816]{1,0:T(8,128)}, bf16[2816,2048]{1,0:T(8,128)(2,1)}, bf16[1024,2048]{1,0:T(8,128)(2,1)}, bf16[2048,1024...) custom-call(bf16[2048,1024]{1,0:T(8,128)(2,1)} %bitcast.2, bf16[2,1024,2816]{2,1,0:T(8,128)(2,1)} %refs_8_.1, ...), custom_call_target="tpu_custom_call" | custom-call | tf_op jit(solution)/shard_map/forward/pallas_call | solution.py:278
  52.7 122.2 %top.1 = (bf16[128,2816]{1,0:T(8,128)(2,1)}, bf16[128,2816]{1,0:T(8,128)(2,1)}, bf16[352,1024]{1,0:T(8,128)(2,1)}, f32[8,128]{1,0:T(8,128)}, bf16[2048,1024]{1,0...) custom-call(bf16[2048,1024]{1,0:T(8,128)(2,1)} %get-tuple-element.34.refs_0_, ...), custom_call_target="tpu_custom_call" | custom-call | tf_op jit(solution)/shard_map/top/pallas_call | solution.py:636
  174.9 82.4 %bottom.1 = (bf16[128,2816]{1,0:T(8,128)(2,1)}, bf16[128,2816]{1,0:T(8,128)(2,1)}, bf16[352,1024]{1,0:T(8,128)(2,1)}, f32[8,128]{1,0:T(8,128)}) custom-call(bf16[2048,1024]{1,0:T(8,128)(2,1)} %get-tuple-element.37.refs_0_, bf16[2816,2048]{1,0:T(8,128)(2,1)} %get-tuple-element.38.refs_1_, bf16[1024,2048]{1,0:T(8,128)(2,1)} %get-tuple-element.39.refs_2_, ...), custom_call_target="tpu_custom_call" | custom-call | tf_op jit(solution)/shard_map/bottom/pallas_call | solution.py:763
  257.3 156.5 %finish.1 = (bf16[2,1024,2816]{2,1,0:T(8,128)(2,1)S(1)}, bf16[2,1024,2816]{2,1,0:T(8,128)(2,1)S(1)}, bf16[2,2816,1024]{2,1,0:T(8,128)(2,1)S(1)}, f32[2,128,2816]...) custom-call(f32[8,128]{1,0:T(8,128)} %get-tuple-element.42.refs_0_, ...), custom_call_target="tpu_custom_call" | custom-call | tf_op jit(solution)/shard_map/finish/pallas_call | solution.py:185
  413.8 16.7 %store.1 = (bf16[2,1024,2816]{2,1,0:T(8,128)(2,1)}, bf16[2,1024,2816]{2,1,0:T(8,128)(2,1)}, bf16[2,2816,1024]{2,1,0:T(8,128)(2,1)}, f32[2,128,2816]{2,1,0:T(8,12...) custom-call(bf16[2,1024,2816]{2,1,0:T(8,128)(2,1)S(1)} %get-tuple-el, ...), custom_call_target="tpu_custom_call" | custom-call | tf_op jit(solution)/shard_map/store/pallas_call | solution.py:198

commit v3 on v2

v3 whole, which is shorter than its diff:
```python
import functools

import jax
import jax.numpy as jnp
from jax import lax
from jax.experimental import pallas as pl
from jax.experimental.pallas import tpu as pltpu
from jax.sharding import PartitionSpec as P

MESH = pl.DeviceIdType.MESH
F32, BF16 = jnp.float32, jnp.bfloat16
CORES = 2
BUFFERS = 2
WEIGHTS = 3
MIB = 2**20
ALL_VMEM = 67043328
TRANSPOSED = ((1,), (1,))


def turn(t):
    return lax.rem(t, BUFFERS)


def repeat(low, high, body):
    def step(i, nothing):
        body(i)
        return nothing

    lax.fori_loop(low, high, step, None)


def split(refs, *sizes):
    left = iter(refs)
    runs = [[next(left) for _ in range(size)] for size in sizes]
    return *runs, list(left)


def local_copies(pairs, sem, *at):
    return [pltpu.make_async_copy(src, dst, sem.at[(k, *at)]) for k, (src, dst) in enumerate(pairs)]


def places(axis, n):
    me = lax.axis_index(axis)
    chips = n // CORES
    core, chip = lax.rem(me, CORES), lax.div(me, CORES)
    at = lambda away: lax.rem(chip + away, chips) * CORES + core
    return me, core, me + 1 - 2 * core, at(1), at(chips - 1), at(2)


class Spread:
    KINDS = 9

    def __init__(self, n, send, recv):
        self.send, self.recv = send, recv
        self.me, _, self.partner, self.after, self.before, self.across = places("dp", n)

    @staticmethod
    def semaphores(pieces):
        return [pltpu.SemaphoreType.DMA((Spread.KINDS, pieces))] * 2

    def barrier(self):
        barrier = pltpu.get_barrier_semaphore()
        for peer in (self.partner, self.after, self.before):
            pl.semaphore_signal(barrier, inc=1, device_id={"dp": peer}, device_id_type=MESH)
        pl.semaphore_wait(barrier, 3)

    def copies(self, number, place, width, own=None, far=None):
        far = far or place
        every, left, right = pl.ds(0, width), pl.ds(0, width // 2), pl.ds(width // 2, width // 2)

        class Copies(dict):
            def __missing__(_, kind):
                to, src, dst = routes[kind]
                sems = (t.at[list(routes).index(kind), number] for t in (self.send, self.recv))
                return pltpu.make_async_remote_copy(src, dst, *sems, device_id={"dp": to}, device_id_type=MESH)

        me, after, before, across = self.me, self.after, self.before, self.across
        own = place(me, every) if own is None else own
        routes = {
            "after": (after, own, place(me, every)),
            "before": (before, own, place(me, every)),
            "partner": (self.partner, own, place(me, every)),
            "on": (after, place(before, left), far(before, left)),
            "back": (before, place(after, right), far(after, right)),
            "partner_before": (self.partner, place(before, every), far(before, every)),
            "partner_after": (self.partner, place(after, every), far(after, every)),
            "partner_left": (self.partner, far(across, left), far(across, left)),
            "partner_right": (self.partner, far(across, right), far(across, right)),
        }
        return Copies()

    @staticmethod
    def start(copies):
        for kind in ("after", "before", "partner"):
            copies[kind].start()

    @staticmethod
    def pass_on(copies):
        copies["after"].wait_recv()
        copies["on"].start()
        copies["partner_before"].start()
        copies["before"].wait_recv()
        copies["back"].start()
        copies["partner_after"].start()

    @staticmethod
    def pass_last(copies):
        copies["on"].wait_recv()
        copies["partner_left"].start()
        copies["back"].wait_recv()
        copies["partner_right"].start()

    @staticmethod
    def end(copies):
        for kind in ("partner", "partner_before", "partner_after", "partner_left", "partner_right"):
            copies[kind].wait_recv()
        for kind in (*Spread.NEAR, *Spread.THEN, *Spread.LAST):
            copies[kind].wait_send()


    NEAR, THEN, LAST = ("after", "before", "partner"), ("on", "back", "partner_before", "partner_after"), ("partner_left", "partner_right")

    @staticmethod
    def end_near(copies):
        for kind in Spread.NEAR:
            copies[kind].wait()

    @staticmethod
    def start_far(copies):
        for kind in Spread.THEN:
            copies[kind].start()

    @staticmethod
    def end_far(copies):
        for kind in Spread.THEN:
            copies[kind].wait_send()
        for kind in (*Spread.THEN[2:], *Spread.LAST):
            copies[kind].wait_recv()
        for kind in Spread.LAST:
            copies[kind].wait_send()


EARLY = ((0, 32), (1, 32))


def finish_kernel(n, count, layers, pieces, *refs):
    some = len(EARLY)
    squares, *g_in = zip(*[iter(refs[: layers + layers * WEIGHTS])] * layers)
    refs = refs[layers + layers * WEIGHTS :]
    w_in, m_in, v_in, near_m, near_v, far_m, far_v, near_g, w, m, v, far_g, g, refs = split(
        refs, *[WEIGHTS] * 3, *[some] * 5, *[WEIGHTS] * 3, some, WEIGHTS
    )
    parts, m_tile, v_tile, g_tile, load_sem, early_sem, tile_sem, part_send, part_recv, send, recv = refs
    spread = Spread(n, send, recv)
    me = spread.me

    barrier = pltpu.get_barrier_semaphore()
    peers = [lax.rem(me + away, n) for away in range(1, n)]
    for peer in peers:
        pl.semaphore_signal(barrier, inc=1, device_id={"dp": peer}, device_id_type=MESH)

    def rows_of(i, owner, first, rows):
        return pl.ds(pl.multiple_of(owner * g[i].shape[1] + first, 16), rows)

    order = (2, 0, 1)
    loads = {}
    for i in order:
        rows = rows_of(i, me, 0, g[i].shape[1])
        pairs = [(w_in[i].at[:, rows], w[i].at[:, rows]), (m_in[i], m[i]), (v_in[i], v[i])]
        pairs += [(g_in[i][k], g[i].at[k]) for k in range(layers)]
        loads[i] = [pltpu.make_async_copy(src, dst, load_sem.at[i, k]) for k, (src, dst) in enumerate(pairs)]
    first_weight, *other_weights = order
    for one in loads[first_weight]:
        one.start()

    total = sum(t[...] for t in squares)
    parts[pl.ds(me, 1)] = total[None]
    early = []
    for k, (i, some) in enumerate(EARLY):
        near = lambda owner, columns, ref=near_g[k]: ref.at[owner, :, columns]
        far = lambda owner, columns, ref=far_g[k]: ref.at[owner, :, columns]
        early.append(spread.copies(len(pieces) + k, near, g[i].shape[2], None, far))
    pl.semaphore_wait(barrier, n - 1)
    part_copies = []
    for k, peer in enumerate(peers):
        part_copies.append(
            pltpu.make_async_remote_copy(
                parts.at[me], parts.at[me], part_send.at[k], part_recv.at[k], device_id={"dp": peer}, device_id_type=MESH
            )
        )
        part_copies[-1].start()
    for copies in early:
        spread.start_far(copies)
    for one in part_copies:
        one.wait_recv()
    every = parts[0]
    for k in range(1, n):
        every += parts[k]
    mean = jnp.sum(every, keepdims=True) / count
    factor = jnp.minimum(1.0, 0.5 * lax.rsqrt(mean + 1e-30))

    def stepped(grad, m_old, v_old, w_old):
        grad = grad.astype(F32) * factor
        m_new = 0.9 * m_old + 0.1 * grad
        v_new = 0.95 * v_old + 0.05 * grad * grad
        w_old = w_old.astype(F32)
        return m_new, v_new, (w_old - 0.02 * (m_new * lax.rsqrt(v_new + 1e-8) + 0.1 * w_old)).astype(BF16)

    step_rows, width = 16, 256

    def adamw(i, layer, first, rows):
        def body(step):
            start = first + step * step_rows
            at = (layer, pl.ds(pl.multiple_of(start, 16), step_rows), slice(None))
            mine = (layer, rows_of(i, me, start, step_rows), slice(None))
            m[i][at], v[i][at], w[i][mine] = stepped(g[i][at], m[i][at], v[i][at], w[i][mine])

        repeat(0, rows // step_rows, body)

    waited = set()

    def compute(i, layer, first, rows):
        if i not in waited:
            waited.add(i)
            for one in loads[i]:
                one.wait()
        adamw(i, layer, first, rows)

    made = []
    for number, (i, layer, first, rows) in enumerate(pieces):
        place = lambda owner, columns, i=i, layer=layer, first=first, rows=rows: w[i].at[layer, rows_of(i, owner, first, rows), columns]
        made.append(spread.copies(number, place, g[i].shape[2]))

    def own_piece(number):
        compute(*pieces[number])
        spread.start(made[number])

    other = lambda device: device + spread.partner - me
    units = []
    for k, (i, some) in enumerate(EARLY):
        near, far = (near_m[k], near_v[k], near_g[k]), (far_m[k], far_v[k], far_g[k])
        for refs, owners in (
            (near, (spread.partner, spread.after, spread.before)),
            (far, (other(spread.after), other(spread.before), spread.across, other(spread.across))),
        ):
            units += [(refs, i, owner, first, g[i].shape[1] - some) for owner in owners for first in range(0, some, step_rows)]

    def unit_loads(number):
        refs, _, owner, first, _ = units[number]
        slot = number % BUFFERS
        tiles = zip(refs, (m_tile, v_tile, g_tile), strict=True)
        return local_copies([(src.at[owner, pl.ds(first, step_rows)], dst.at[slot]) for src, dst in tiles], tile_sem, slot)

    def unit_rows(number):
        _, i, owner, first, start = units[number]
        return rows_of(i, owner, start + first, step_rows)

    last = layers - 1
    old_rows = local_copies(
        [tuple(t[i].at[last, unit_rows(number)] for t in (w_in, w)) for number, (_, i, _, _, _) in enumerate(units)], early_sem
    )

    def unit(number):
        (_, i, _, _, _), slot = units[number], number % BUFFERS
        if number + 1 < len(units):
            for one in unit_loads(number + 1):
                one.start()
        for one in (*unit_loads(number), old_rows[number]):
            one.wait()

        def body(step):
            columns = pl.ds(pl.multiple_of(step * width, width), width)
            its, at = (last, unit_rows(number), columns), (slot, slice(None), columns)
            *_, w[i][its] = stepped(g_tile[at], m_tile[at], v_tile[at], w[i][its])

        repeat(0, g[i].shape[-1] // width, body)

    own_piece(0)
    for i in other_weights:
        for one in loads[i]:
            one.start()
    for one in old_rows:
        one.start()
    total_pieces, done = len(pieces), 0
    for number in range(total_pieces + 2):
        if number + 1 < total_pieces:
            own_piece(number + 1)
        if number == 0:
            for copies in early:
                spread.pass_last(copies)
        if 1 <= number <= total_pieces:
            spread.pass_on(made[number - 1])
        if 2 <= number:
            spread.pass_last(made[number - 2])
        if number == 2:
            for copies in early:
                spread.end_far(copies)
            for one in unit_loads(0):
                one.start()
        if 3 <= number < total_pieces:
            for k in range(min(3, len(units) - done)):
                unit(done + k)
            done += min(3, len(units) - done)
    for k in range(done, len(units)):
        unit(k)
    for i, some in EARLY:
        compute(i, last, g[i].shape[1] - some, some)
    for copies in made:
        spread.end(copies)
    for one in part_copies:
        one.wait_send()


def store_kernel(*refs):
    *refs, sem = refs
    some = len(refs) // 2
    copies = local_copies([(refs[k], refs[some + k]) for k in range(some)], sem)
    for one in copies:
        one.start()
    for one in copies:
        one.wait()


def early_shapes(n, blocks, dtype, times=1):
    return [jax.ShapeDtypeStruct((n, some, blocks[i][0].shape[-1]), dtype) for _ in range(times) for i, some in EARLY]


def finish(n, gradients, squares, weights, m, v, early):
    count = float(sum(w.size for w in weights))
    layers = len(gradients[0])
    pieces = []
    for i in (2, 0, 1):
        rows, _ = gradients[i][0].shape
        for layer in range(layers):
            half = rows // 2
            cuts = [half, half]
            if (i, layer) == (2, 0):
                cuts = [48, half - 48, half]
            elif layer == layers - 1 and i in dict(EARLY):
                rest = half - dict(EARLY)[i]
                cuts = [half, rest - 16, 16] if i == 1 else [half, rest]
            for cut in cuts:
                pieces.append((i, layer, sum(p[3] for p in pieces if p[:2] == (i, layer)), cut))
    anywhere, inside = pl.BlockSpec(memory_space=pl.ANY), pl.BlockSpec(memory_space=pltpu.VMEM)
    dma = pltpu.SemaphoreType.DMA
    results = [*weights, *m, *v]
    tile = lambda dtype: pltpu.VMEM((BUFFERS, 16, max(gradients[i][0].shape[1] for i, _ in EARLY)), dtype)
    ready = pl.pallas_call(
        functools.partial(finish_kernel, n, count, layers, tuple(pieces)),
        out_shape=[pltpu.VMEM(t.shape, t.dtype) for t in results]
        + early_shapes(n, gradients, BF16),
        in_specs=[inside] * layers + [anywhere] * (WEIGHTS * layers + len(results) + len(early)),
        out_specs=[inside] * len(results) + [anywhere] * len(EARLY),
        scratch_shapes=[
            *[pltpu.VMEM((layers, *one[0].shape), BF16) for one in gradients],
            pltpu.VMEM((n, 8, 128), F32), tile(F32), tile(F32), tile(BF16),
            dma((WEIGHTS, layers + 3)), dma((sum(some for _, some in EARLY) // 16 * (n - 1),)), dma((3, BUFFERS)), *[dma((n - 1,))] * 2,
            *Spread.semaphores(len(pieces) + len(EARLY)),
        ],
        compiler_params=pltpu.CompilerParams(collective_id=4, has_side_effects=True, vmem_limit_bytes=8 * MIB),
        name="finish",
    )(*squares, *sum(gradients, ()), *weights, *m, *v, *early)[: len(results)]
    return pl.pallas_call(
        store_kernel,
        out_shape=[jax.ShapeDtypeStruct(t.shape, t.dtype) for t in results],
        in_specs=[inside] * len(results),
        out_specs=[anywhere] * len(results),
        scratch_shapes=[dma((len(results),))],
        compiler_params=pltpu.CompilerParams(vmem_limit_bytes=8 * MIB),
        name="store",
    )(*[pltpu.with_memory_space_constraint(t, pltpu.VMEM) for t in ready])


def dot(a, b, contract=((1,), (0,))):
    return lax.dot_general(a, b, (contract, ((), ())), preferred_element_type=F32)


def normed(h):
    wide = h.astype(F32)
    return (wide * lax.rsqrt(jnp.mean(wide * wide, -1, keepdims=True) + 1e-6)).astype(BF16)


def by_norm(h, by_a):
    wide = h.astype(F32)
    scale = lax.rsqrt(jnp.mean(wide * wide, -1, keepdims=True) + 1e-6)
    return scale * by_a - wide * (scale * scale * scale * jnp.mean(by_a * wide, -1, keepdims=True))


def by_units(gate, up, by_hidden):
    by_hidden = by_hidden.astype(BF16).astype(F32)
    s = jax.nn.sigmoid(gate)
    silu = gate * s
    return silu * up, by_hidden * up * (s + silu * (1.0 - s)), by_hidden * silu


def forward_kernel(n, *refs):
    (x_in, w_gate, w_up, w_down), moments, outs, early, refs = split(refs, 4, 2 * len(EARLY), 7, 2 * len(EARLY))
    gate_out, up_out, ht_out, at_out, h_out, b_out, bt_out = outs
    (wg, wu, wd, hidden, x, gate, up, hidden_t, a_t, h, b, b_t, w_sem, x_sem, sem, late_sem, send, recv) = refs
    spread = Spread(n, send, recv)
    rows = x.shape[1]
    tiles = x_in.shape[0] // rows
    ff = wg.shape[1]
    width = 256
    groups = [range(at, min(at + 3 * width, ff), width) for at in range(0, ff, 3 * width)]
    tall = lambda ref, t: ref.at[pl.ds(pl.multiple_of(t * rows, rows), rows)]
    wide = lambda ref, t: ref.at[:, pl.ds(pl.multiple_of(t * rows, rows), rows)]

    def load_x(t):
        return pltpu.make_async_copy(tall(x_in, t), x.at[lax.rem(t, x.shape[0])], x_sem.at[lax.rem(t, x.shape[0])])

    def stores(t, first):
        slot = turn(t)
        if first:
            pairs = [(gate, tall(gate_out, t)), (up, tall(up_out, t)), (hidden_t, wide(ht_out, t)), (a_t, wide(at_out, t))]
        else:
            pairs = [(h, tall(h_out, t)), (b, tall(b_out, t)), (b_t, wide(bt_out, t))]
        return local_copies([(src.at[slot], dst) for src, dst in pairs], sem if first else late_sem, slot)

    w_loads = []
    for k, group in enumerate(groups):
        columns = slice(group[0], group[-1] + width)
        w_loads.append([
            pltpu.make_async_copy(src.at[0, :, columns], dst.at[:, columns], w_sem.at[j, k]) for j, (src, dst) in enumerate(((w_gate, wg), (w_up, wu)))
        ])
    down_load = pltpu.make_async_copy(w_down.at[0], wd, w_sem.at[2, 0])
    for one in (load_x(0), *w_loads[0], *w_loads[1], load_x(1)):
        one.start()
    spread.barrier()
    pieces = []
    for number, (src, dst) in enumerate(zip(moments, early, strict=True)):
        some = dst.shape[1]
        own = src.at[src.shape[0] - 1, pl.ds(src.shape[1] - some, some)]
        pieces.append(spread.copies(number, lambda owner, columns, dst=dst: dst.at[owner, :, columns], dst.shape[2], own))
    for copies in pieces:
        spread.start(copies)

    def first_part(t, group, a):
        slot = turn(t)
        for at in group:
            columns = slice(at, at + width)
            g, u = dot(a, wg[:, columns]), dot(a, wu[:, columns])
            gate[slot, :, columns] = g
            up[slot, :, columns] = u
            units = (g * jax.nn.sigmoid(g) * u).astype(BF16)
            hidden[:, columns] = units
            hidden_t[slot, columns] = units.T

    def second_part(t):
        slot = turn(t)
        out = x[lax.rem(t, x.shape[0])] + dot(hidden[...], wd[...]).astype(BF16)
        h[slot] = out
        after = normed(out)
        b[slot] = after
        b_t[slot] = after.T

    def normed_tile(t):
        a = normed(x[lax.rem(t, x.shape[0])])
        a_t[turn(t)] = a.T
        return a

    load_x(0).wait()
    a = normed_tile(0)
    for k, group in enumerate(groups):
        for one in w_loads[k]:
            one.wait()
        for one in w_loads[k + 2] if k + 2 < len(groups) else ([down_load] if k + 2 == len(groups) else []):
            one.start()
        first_part(0, group, a)
    for one in stores(0, True):
        one.start()
    down_load.wait()

    def tile(t):
        load_x(t).wait()

        @pl.when(t + 1 < tiles)
        def _():
            load_x(t + 1).start()

        @pl.when(t >= BUFFERS)
        def _():
            for one in stores(t - BUFFERS, True):
                one.wait()

        @pl.when(t > BUFFERS)
        def _():
            for one in stores(t - 1 - BUFFERS, False):
                one.wait()

        a = normed_tile(t)
        second_part(t - 1)
        first_part(t, range(0, ff, width), a)
        for one in (*stores(t - 1, False), *stores(t, True)):
            one.start()

    repeat(1, tiles, tile)
    last = tiles - 1
    for one in stores(last - BUFFERS, False):
        one.wait()
    second_part(last)
    for one in stores(last, False):
        one.start()
    for copies in pieces:
        spread.end_near(copies)
    for t in (last - 1, last):
        for one in (*stores(t, True), *stores(t, False)):
            one.wait()


def layer_0(n, x, w_gate, w_up, w_down, m, v):
    tokens, d = x.shape
    ff = w_gate.shape[2]
    rows = 256
    anywhere = pl.BlockSpec(memory_space=pl.ANY)
    dma = pltpu.SemaphoreType.DMA
    vmem = lambda *shape: pltpu.VMEM(shape, BF16)
    return pl.pallas_call(
        functools.partial(forward_kernel, n),
        in_specs=[anywhere] * (4 + 2 * len(EARLY)),
        out_specs=[anywhere] * (7 + 2 * len(EARLY)),
        out_shape=[
            jax.ShapeDtypeStruct((tokens, ff), F32),
            jax.ShapeDtypeStruct((tokens, ff), F32),
            jax.ShapeDtypeStruct((ff, tokens), BF16),
            jax.ShapeDtypeStruct((d, tokens), BF16),
            jax.ShapeDtypeStruct((tokens, d), BF16),
            jax.ShapeDtypeStruct((tokens, d), BF16),
            jax.ShapeDtypeStruct((d, tokens), BF16),
            *early_shapes(n, m, F32, 2),
        ],
        scratch_shapes=[
            vmem(d, ff), vmem(d, ff), vmem(ff, d), vmem(rows, ff), vmem(3, rows, d),
            *[pltpu.VMEM((BUFFERS, rows, ff), F32)] * 2, *[vmem(BUFFERS, *t) for t in ((ff, rows), (d, rows), (rows, d), (rows, d), (d, rows))],
            dma((WEIGHTS, 4)), dma((3,)), dma((4, BUFFERS)), dma((3, BUFFERS)), *Spread.semaphores(2 * len(EARLY)),
        ],
        compiler_params=pltpu.CompilerParams(collective_id=1, has_side_effects=True, vmem_limit_bytes=60 * MIB),
        name="forward",
    )(x, w_gate, w_up, w_down, *[t[i] for t in (m, v) for i, _ in EARLY])


class Exchange:
    def __init__(self, n, refs, kinds, lags):
        self.mine, self.pair, self.out2, self.out3, self.in2, self.in3, self.own, self.side, self.pair_sem, self.sem2, self.sem3 = refs
        self.kinds = kinds
        self.lags = lags
        self.me, self.core, self.partner, self.after, self.before, _ = places("dp", n)
        chips = n // CORES
        self.chip = lax.div(self.me, CORES)
        self.chip_after, self.chip_before, self.chip_across = (lax.rem(self.chip + k, chips) for k in (1, chips - 1, chips // 2))
        half = self.out3.shape[-1]
        self.left, self.right = slice(0, half), slice(half, 2 * half)

    @staticmethod
    def scratch(n, rows, width, lags):
        chips, half, dma = n // CORES, width // 2, pltpu.SemaphoreType.DMA
        _, two, three, four = lags
        slots1, slots2, slots3 = two + 3, 2 * (three - two) + 2, 2 * (four - three) + 2
        return [
            pltpu.VMEM((two + 1, chips, CORES, rows, width), BF16),
            pltpu.VMEM((slots1, chips, rows, width), BF16),
            pltpu.VMEM((2, three - two + 1, rows, width), BF16),
            pltpu.VMEM((2, four - three + 1, rows, half), BF16),
            pltpu.VMEM((2, slots2, rows, width), BF16),
            pltpu.VMEM((2, slots3, rows, half), BF16),
            pltpu.VMEM((four - two + 1, rows, width), F32),
            pltpu.VMEM((2, three - two + 1, rows, half), F32),
            dma((2, slots1)), dma((2, 2, slots2)), dma((2, 2, slots3)),
        ]

    def held(self, p):
        return lax.rem(p, self.mine.shape[0])

    def barrier(self):
        barrier = pltpu.get_barrier_semaphore()
        for peer in (self.partner, self.after, self.before):
            pl.semaphore_signal(barrier, inc=1, device_id={"dp": peer}, device_id_type=MESH)
        pl.semaphore_wait(barrier, 3)

    def copy1(self, p, rows):
        slot = lax.rem(p, self.pair.shape[0])
        return pltpu.make_async_remote_copy(
            self.mine.at[self.held(p), :, 1 - self.core, pl.ds(0, rows)], self.pair.at[slot, :, pl.ds(0, rows)],
            self.pair_sem.at[0, slot], self.pair_sem.at[1, slot], device_id={"dp": self.partner}, device_id_type=MESH,
        )

    def copies(self, p, rows, out, into, sem):
        slot = lax.rem(p, into.shape[1])
        return [
            pltpu.make_async_remote_copy(
                out.at[way, lax.rem(p, out.shape[1]), pl.ds(0, rows)], into.at[way, slot, pl.ds(0, rows)],
                sem.at[0, way, slot], sem.at[1, way, slot], device_id={"dp": to}, device_id_type=MESH,
            )
            for way, to in enumerate((self.after, self.before))
        ]

    def copies2(self, p, rows):
        return self.copies(p, rows, self.out2, self.in2, self.sem2)

    def copies3(self, p, rows):
        return self.copies(p, rows, self.out3, self.in3, self.sem3)

    def stage1(self, p, rows, _):
        self.copy1(p, rows).start()

    def stage2(self, p, rows, _):
        self.copy1(p, rows).wait()
        slot, own, side = (lax.rem(p, t.shape[k]) for t, k in ((self.out2, 1), (self.own, 0), (self.side, 1)))
        at = slice(0, rows)

        def of_chip(chip, columns):
            a = self.mine[self.held(p), chip, self.core, at, columns].astype(F32)
            return a + self.pair[lax.rem(p, self.pair.shape[0]), chip, at, columns].astype(F32)

        self.out2[0, slot, at, self.left] = of_chip(self.chip_across, self.left).astype(BF16)
        self.out2[0, slot, at, self.right] = of_chip(self.chip_after, self.right).astype(BF16)
        self.out2[1, slot, at, self.left] = of_chip(self.chip_before, self.left).astype(BF16)
        self.out2[1, slot, at, self.right] = of_chip(self.chip_across, self.right).astype(BF16)
        for one in self.copies2(p, rows):
            one.start()
        self.side[0, side, at] = of_chip(self.chip_after, self.left)
        self.side[1, side, at] = of_chip(self.chip_before, self.right)
        for columns in (self.left, self.right):
            self.own[own, at, columns] = of_chip(self.chip, columns)

    def stage3(self, p, rows, _):
        for one in self.copies2(p, rows):
            one.wait()
        slot, arrived, own, side = (lax.rem(p, t.shape[k]) for t, k in ((self.out3, 1), (self.in2, 1), (self.own, 0), (self.side, 1)))
        at = slice(0, rows)
        self.out3[0, slot, at] = (self.side[0, side, at] + self.in2[0, arrived, at, self.left].astype(F32)).astype(BF16)
        self.out3[1, slot, at] = (self.side[1, side, at] + self.in2[1, arrived, at, self.right].astype(F32)).astype(BF16)
        for one in self.copies3(p, rows):
            one.start()
        self.own[own, at, self.left] += self.in2[1, arrived, at, self.left].astype(F32)
        self.own[own, at, self.right] += self.in2[0, arrived, at, self.right].astype(F32)

    def stage4(self, p, rows, keep):
        for one in self.copies3(p, rows):
            one.wait()
        arrived, own = lax.rem(p, self.in3.shape[1]), lax.rem(p, self.own.shape[0])
        at = slice(0, rows)
        a = self.own[own, at, self.left] + self.in3[0, arrived, at].astype(F32)
        b = self.own[own, at, self.right] + self.in3[1, arrived, at].astype(F32)
        keep(p, a.astype(BF16), b.astype(BF16))

    def finish(self, step, packets):
        for step in range(step, packets + self.lags[-1]):
            self.move(step, step, step + 1)

    def move(self, step, low, high):
        for lag, stage in zip(self.lags, (self.stage1, self.stage2, self.stage3, self.stage4), strict=True):
            for first, end, rows, keep in self.kinds:
                if high - 1 - lag < first or low - lag >= end:
                    continue
                p = step - lag
                if low - lag >= first and high - 1 - lag < end:
                    stage(p, rows, keep)
                else:
                    pl.when((p >= first) & (p < end))(functools.partial(stage, p, rows, keep))


def add_squares(total, *blocks):
    for block in blocks:
        wide = block.astype(F32)
        wide = wide * wide
        rows, columns = wide.shape
        sums = [wide[r : r + 8, c : c + 128] for r in range(0, rows, 8) for c in range(0, columns, 128)]
        while len(sums) > 1:
            sums = [a + b for a, b in zip(sums[::2], sums[1::2])] + ([sums[-1]] if len(sums) % 2 else [])
        total[...] += sums[0]


def keep_columns(first, gate, up, width, squares):
    def keep(p, left, right):
        columns = pl.ds(pl.multiple_of((p - first) * width, width), width)
        gate[:, columns] = left
        up[:, columns] = right
        add_squares(squares, left, right)

    return keep


def keep_down(first, down, rows, width, squares):
    def keep(p, left, right):
        half = width // 2
        which = p - first
        at = pl.ds(pl.multiple_of(lax.rem(which, 2) * rows, 16), rows)
        start = lax.div(which, 2) * width
        down[at, pl.ds(pl.multiple_of(start, half), half)] = left
        down[at, pl.ds(pl.multiple_of(start + half, half), half)] = right
        add_squares(squares, left, right)

    return keep


def down_packet(exchange, step, first, hidden_t, by_out):
    n_rows = hidden_t.shape[0]
    _, chips, cores, rows, width = exchange.mine.shape
    which = step - first
    start = pl.multiple_of(lax.rem(which, 2) * rows, 16)
    columns = pl.ds(pl.multiple_of(lax.div(which, 2) * width, width), width)
    share = n_rows // (chips * cores)
    by_out = by_out[:, columns]
    for k in range(chips * cores):
        lhs = hidden_t[pl.ds(pl.multiple_of(k * share + start, 16), rows), :]
        exchange.mine[exchange.held(step), k // cores, k % cores] = dot(lhs, by_out).astype(BF16)


def wide_packet(exchange, step, a_t, by_both):
    _, chips, cores, _, width = exchange.mine.shape
    rows = a_t.shape[0] // (chips * cores)
    half = width // 2
    for k in range(2):
        columns = slice(k * half, k * half + half)
        block = dot(a_t[...], by_both[:, columns]).astype(BF16)
        exchange.mine[exchange.held(step), :, :, pl.ds(0, rows), columns] = block.reshape(chips, cores, rows, half)


MB = 512
LAGS = (0, 1, 3, 5)


def top_kernel(n, *refs):
    several = 2 * len(EARLY)
    ins, near, outs, far, (send, recv), refs = split(refs, 7, several, 7, several, 2)
    a_in, at_in, h_in, dy_in, w_gate, w_up, w_down = ins
    g_gate, g_up, g_down, squares, by_h, bg_hbm, bu_hbm = outs
    spread = Spread(n, send, recv)
    (a, a_t, dy, wg, wu, hidden_t, wd, both, h_tile, by_tile, load_sem, wd_sem, both_sem, tile_sem, by_sem), refs = split(refs, 15)
    tokens, d = a.shape
    ff = wg.shape[1]
    width = 256
    chunks = ff // width
    downs = 4
    wide_rows, down_rows = d // n, ff // n // 2
    exchange = Exchange(
        n, refs,
        (
            (0, chunks, wide_rows, keep_columns(0, g_gate, g_up, width, squares)),
            (chunks, chunks + downs, down_rows, keep_down(chunks, g_down, down_rows, 2 * width, squares)),
        ),
        LAGS,
    )
    layer = w_gate.shape[0] - 1
    first, rest = pl.ds(0, width), pl.ds(width, ff - width)
    columns_of = lambda columns: [(src.at[layer, :, columns], dst.at[:, columns]) for src, dst in ((w_gate, wg), (w_up, wu))]
    loads = local_copies([(a_in, a), (dy_in, dy), (at_in, a_t), *columns_of(first), *columns_of(rest)], load_sem)
    def down_chunk(c):
        slot = turn(c)
        return pltpu.make_async_copy(w_down.at[layer, pl.ds(pl.multiple_of(c * width, width), width)], wd.at[slot], wd_sem.at[slot])

    loads, later_loads = split(loads, 5)
    for one in (*loads, down_chunk(0)):
        one.start()
    squares[...] = jnp.zeros_like(squares)
    exchange.barrier()

    early = []
    for number, (src, dst) in enumerate(zip(near, far, strict=True)):
        places = [lambda owner, columns, ref=ref: ref.at[owner, :, columns] for ref in (src, dst)]
        early.append(spread.copies(number, places[0], src.shape[2], None, places[1]))
    for copies in early:
        spread.start_far(copies)

    def store_both(c):
        slot = turn(c)
        to = pl.ds(pl.multiple_of(c * width, width), width)
        return local_copies([(both.at[slot, :, pl.ds(k * width, width)], ref.at[:, to]) for k, ref in enumerate((bg_hbm, bu_hbm))], both_sem, slot)

    def chunk(c):
        slot = turn(c)

        @pl.when(c == 0)
        def _():
            for one in loads:
                one.wait()
            for one in later_loads:
                one.start()

        @pl.when(c == 1)
        def _():
            for one in later_loads:
                one.wait()

        @pl.when(c >= BUFFERS)
        def _():
            for one in store_both(c - BUFFERS):
                one.wait()

        @pl.when(c == chunks // 2)
        def _():
            for copies in early:
                spread.pass_last(copies)

        down_chunk(c).wait()

        @pl.when(c + 1 < chunks)
        def _():
            down_chunk(c + 1).start()

        columns = pl.ds(pl.multiple_of(c * width, width), width)
        wg_c, wu_c, wd_c = wg[:, columns], wu[:, columns], wd[slot]
        for at in range(0, tokens, MB):
            rows = slice(at, at + MB)
            hidden, by_gate, by_up = by_units(dot(a[rows], wg_c), dot(a[rows], wu_c), dot(dy[rows], wd_c, TRANSPOSED))
            hidden_t[columns, rows] = hidden.astype(BF16).T
            both[slot, rows, :width] = by_gate.astype(BF16)
            both[slot, rows, width:] = by_up.astype(BF16)
        wide_packet(exchange, c, a_t, both.at[slot])
        for one in store_both(c):
            one.start()
        exchange.move(c, 0, chunks)

    repeat(0, chunks, chunk)
    for c in range(chunks - BUFFERS, chunks):
        for one in store_both(c):
            one.wait()

    tile_rows = 256
    tiles = tokens // tile_rows
    split_at = a_t.shape[1]

    def tile_loads(t):
        slot = turn(t)
        rows = pl.ds(pl.multiple_of(t * tile_rows, tile_rows), tile_rows)
        pairs = [(h_in.at[rows], h_tile.at[slot])]
        for k, src in enumerate((bg_hbm, bu_hbm)):
            to = pl.ds(pl.multiple_of((slot * 2 + k) * tile_rows, tile_rows), tile_rows)
            pairs.append((src.at[rows, pl.ds(0, split_at)], a_t.at[to]))
            pairs.append((src.at[rows, pl.ds(split_at, ff - split_at)], a.at[to, pl.ds(0, ff - split_at)]))
        return local_copies(pairs, tile_sem, slot)

    def tile_store(t):
        slot = turn(t)
        return pltpu.make_async_copy(by_tile.at[slot], by_h.at[pl.ds(pl.multiple_of(t * tile_rows, tile_rows), tile_rows)], by_sem.at[slot])

    for one in tile_loads(0):
        one.start()

    def tile(step):
        t = step - chunks

        @pl.when(t < downs)
        def _():
            down_packet(exchange, step, chunks, hidden_t, dy)

        exchange.move(step, chunks, chunks + tiles)
        slot = turn(t)
        for one in tile_loads(t):
            one.wait()

        @pl.when(t + 1 < tiles)
        def _():
            for one in tile_loads(t + 1):
                one.start()

        @pl.when(t >= BUFFERS)
        def _():
            tile_store(t - BUFFERS).wait()

        total = None
        for k, w in enumerate((wg, wu)):
            at = pl.ds(pl.multiple_of((slot * 2 + k) * tile_rows, tile_rows), tile_rows)
            term = dot(a_t[at], w[:, :split_at], TRANSPOSED) + dot(a[at, : ff - split_at], w[:, split_at:], TRANSPOSED)
            total = term if total is None else total + term
        rows = pl.ds(pl.multiple_of(t * tile_rows, tile_rows), tile_rows)
        by_tile[slot] = (dy[rows].astype(F32) + by_norm(h_tile[slot], total)).astype(BF16)
        tile_store(t).start()

    repeat(chunks, chunks + tiles, tile)
    exchange.finish(chunks + tiles, chunks + downs)
    for t in range(tiles - BUFFERS, tiles):
        tile_store(t).wait()
    for copies in early:
        spread.end_far(copies)


def top_layer(n, a, a_t, h, dy, w_gate, w_up, w_down, near):
    tokens, d = a.shape
    ff = w_gate.shape[2]
    width = 256
    anywhere, inside = pl.BlockSpec(memory_space=pl.ANY), pl.BlockSpec(memory_space=pltpu.VMEM)
    dma = pltpu.SemaphoreType.DMA
    return pl.pallas_call(
        functools.partial(top_kernel, n),
        in_specs=[anywhere] * (7 + len(near)),
        out_specs=[inside] * 4 + [anywhere] * (3 + len(near)),
        out_shape=[
            jax.ShapeDtypeStruct((d // n, ff), BF16),
            jax.ShapeDtypeStruct((d // n, ff), BF16),
            jax.ShapeDtypeStruct((ff // n, d), BF16),
            jax.ShapeDtypeStruct((8, 128), F32),
            jax.ShapeDtypeStruct((tokens, d), BF16),
            jax.ShapeDtypeStruct((tokens, ff), BF16),
            jax.ShapeDtypeStruct((tokens, ff), BF16),
            *[jax.ShapeDtypeStruct(t.shape, t.dtype) for t in near],
        ],
        scratch_shapes=[
            *Spread.semaphores(len(near)),
            *[pltpu.VMEM(t, BF16) for t in ((tokens, d), (d, tokens), (tokens, d), (d, ff), (d, ff), (ff, tokens))],
            *[pltpu.VMEM((BUFFERS, *t), BF16) for t in ((width, d), (tokens, 2 * width), (width, d), (width, d))],
            dma((7,)), dma((BUFFERS,)), dma((2, BUFFERS)), dma((5, BUFFERS)), dma((BUFFERS,)),
            *Exchange.scratch(n, ff // n // 2, 2 * width, LAGS),
        ],
        compiler_params=pltpu.CompilerParams(collective_id=2, has_side_effects=True, vmem_limit_bytes=ALL_VMEM),
        name="top",
    )(a, a_t, h, dy, w_gate, w_up, w_down, *near)


def bottom_kernel(n, *refs):
    some = len(EARLY)
    ins, summed, (g_gate, g_up, g_down, squares), near, (send, recv), refs = split(refs, 6, some, 4, some, 2)
    by_in, ht_in, at_in, gate_in, up_in, w_down = ins
    spread = Spread(n, send, recv)
    (by, hidden_t, a_t, wd, gate, up, both, load_sem, unit_sem), refs = split(refs, 9)
    tokens, d = by.shape
    ff = hidden_t.shape[0]
    width = 256
    chunks = ff // width
    downs = 4
    wide_rows, down_rows = d // n, ff // n // 2
    exchange = Exchange(
        n, refs,
        (
            (0, downs, down_rows, keep_down(0, g_down, down_rows, 2 * width, squares)),
            (downs, downs + chunks, wide_rows, keep_columns(downs, g_gate, g_up, width, squares)),
        ),
        LAGS,
    )
    share = ff // n
    halves = lambda ref, k: ref.at[:, pl.ds(k * 2 * width, 2 * width)]
    pairs = [(halves(by_in, 0), halves(by, 0))]
    for k in range(2):
        for to in range(n):
            rows = pl.ds(to * share + k * down_rows, down_rows)
            pairs.append((ht_in.at[rows], hidden_t.at[rows]))
    pairs += [(halves(by_in, 1), halves(by, 1)), (at_in, a_t)]
    loads = local_copies(pairs, load_sem)

    def chunk_loads(c):
        slot = turn(c)
        columns = pl.ds(pl.multiple_of(c * width, width), width)
        pairs = [(w_down.at[0, columns], wd.at[slot]), (gate_in.at[:, columns], gate.at[slot]), (up_in.at[:, columns], up.at[slot])]
        return local_copies(pairs, unit_sem, slot)

    first, second, third = split(loads, 1 + n, n)
    third += chunk_loads(0)
    for one in first:
        one.start()
    squares[...] = jnp.zeros_like(squares)
    exchange.barrier()

    early = []
    for number, (src, dst) in enumerate(zip(summed, near, strict=True)):
        some = dst.shape[1]
        own = src.at[pl.ds(src.shape[0] - some, some)]
        early.append(spread.copies(number, lambda owner, columns, dst=dst: dst.at[owner, :, columns], dst.shape[2], own))
    for copies in early:
        spread.start(copies)

    def down(step):
        @pl.when(step == 0)
        def _():
            for one in first:
                one.wait()
            for one in second:
                one.start()

        @pl.when(step == 1)
        def _():
            for one in second:
                one.wait()
            for one in third:
                one.start()

        @pl.when(step == 2)
        def _():
            for one in third[:2]:
                one.wait()

        down_packet(exchange, step, 0, hidden_t, by)
        exchange.move(step, 0, downs)

    repeat(0, downs, down)

    def chunk(step):
        c = step - downs
        slot = turn(c)
        for one in chunk_loads(c):
            one.wait()

        @pl.when(c + 1 < chunks)
        def _():
            for one in chunk_loads(c + 1):
                one.start()

        wd_c = wd[slot]
        for at in range(0, tokens, MB):
            rows = slice(at, at + MB)
            _, by_gate, by_up = by_units(gate[slot, rows], up[slot, rows], dot(by[rows], wd_c, TRANSPOSED))
            both[rows, :width] = by_gate.astype(BF16)
            both[rows, width:] = by_up.astype(BF16)
        wide_packet(exchange, step, a_t, both)
        exchange.move(step, downs, downs + chunks)

    repeat(downs, downs + chunks, chunk)
    exchange.finish(downs + chunks, downs + chunks)
    for copies in early:
        spread.end_near(copies)


def bottom_layer(n, by, hidden_t, a_t, gate, up, w_down, summed):
    tokens, d = by.shape
    ff = hidden_t.shape[0]
    width = 256
    anywhere, inside = pl.BlockSpec(memory_space=pl.ANY), pl.BlockSpec(memory_space=pltpu.VMEM)
    dma = pltpu.SemaphoreType.DMA
    return pl.pallas_call(
        functools.partial(bottom_kernel, n),
        in_specs=[anywhere] * (6 + len(summed)),
        out_specs=[inside] * 4 + [anywhere] * len(summed),
        out_shape=[
            jax.ShapeDtypeStruct((d // n, ff), BF16),
            jax.ShapeDtypeStruct((d // n, ff), BF16),
            jax.ShapeDtypeStruct((ff // n, d), BF16),
            jax.ShapeDtypeStruct((8, 128), F32),
            *[jax.ShapeDtypeStruct((n, some, ff), BF16) for _, some in EARLY],
        ],
        scratch_shapes=[
            *Spread.semaphores(len(summed)),
            *[pltpu.VMEM(t, BF16) for t in ((tokens, d), (ff, tokens), (d, tokens), (BUFFERS, width, d))],
            *[pltpu.VMEM((BUFFERS, tokens, width), F32)] * 2, pltpu.VMEM((tokens, 2 * width), BF16),
            dma((3 + 2 * n,)), dma((3, BUFFERS)),
            *Exchange.scratch(n, ff // n // 2, 2 * width, LAGS),
        ],
        compiler_params=pltpu.CompilerParams(collective_id=3, has_side_effects=True, vmem_limit_bytes=ALL_VMEM),
        name="bottom",
    )(by, hidden_t, a_t, gate, up, w_down, *summed)


def solution(mesh):
    n = mesh.shape["dp"]

    def step(x, dy, w_gate, w_up, w_down, *moments):
        m, v = split(moments, WEIGHTS)
        gate, up, hidden_t, a_t, h, next_a, next_a_t, *early = layer_0(n, x[0], w_gate, w_up, w_down, m, v)
        top = top_layer(n, next_a, next_a_t, h, dy[0], w_gate, w_up, w_down, early)
        top, (squares_1, by_h, _, _), far = split(top, WEIGHTS, 4)
        bottom = bottom_layer(n, by_h, hidden_t, a_t, gate, up, w_down, [top[i] for i, _ in EARLY])
        bottom, (squares_0,), near = split(bottom, WEIGHTS, 1)
        gradients = list(zip(bottom, top, strict=True))
        return tuple(finish(n, gradients, (squares_0, squares_1), (w_gate, w_up, w_down), m, v, (*early, *far, *near)))

    sharded = P(None, "dp", None)
    return jax.shard_map(
        step,
        mesh=mesh,
        in_specs=(P(("rep", "dp")), P(("rep", "dp")), P(), P(), P(), *[sharded] * 6),
        out_specs=(*[P("rep")] * 3, *[P("rep", "dp")] * 6),
        check_vma=False,
    )
```

time: 431 us -> 415 us (0.963)
  Pallas kernels: 430 us -> 414 us
    pallas_call x3, Pallas kernels: 331 us -> 314 us  [the longest x1 145 us: finish(): pl.pallas_call(functools.partial(finish_kernel, n, count, layers, tuple(p...]
where the time goes in v3:
time: 415 us
  Pallas kernels  414 us (100%)
    pallas_call x1, Pallas kernels, finish(): pl.pallas_call(functools.partial(finish_kernel, n, count, layers, tuple(p...  145 us
    pallas_call x1, Pallas kernels, top_layer(): pl.pallas_call(functools.partial(top_kernel, n), in_specs=[anywhere] * (7...  121 us
    pallas_call x1, Pallas kernels, bottom_layer(): pl.pallas_call(functools.partial(bottom_kernel, n), in_specs=[anywhere] *...  83.5 us
    pallas_call x1, Pallas kernels, layer_0(): pl.pallas_call(functools.partial(forward_kernel, n), in_specs=[anywhere]...  47 us
    pallas_call x1, Pallas kernels, finish(): pl.pallas_call(store_kernel, out_shape=[jax.ShapeDtypeStruct(t.shape, t.d...  16.7 us

profile of v3, /device:TPU:113, one launch (start us, length us, event | category | flops | bytes accessed | tf_op | source)
XLA Modules:
  0.0 414.6 jit_solution(7635269260926958560)
XLA Ops:
  0.6 47.0 %forward.1 = (f32[2048,2816]{1,0:T(8,128)}, f32[2048,2816]{1,0:T(8,128)}, bf16[2816,2048]{1,0:T(8,128)(2,1)}, bf16[1024,2048]{1,0:T(8,128)(2,1)}, bf16[2048,1024...) custom-call(bf16[2048,1024]{1,0:T(8,128)(2,1)} %bitcast.2, ...), custom_call_target="tpu_custom_call" | custom-call | tf_op jit(solution)/shard_map/forward/pallas_call | solution.py:518
  47.6 121.4 %top.1 = (bf16[128,2816]{1,0:T(8,128)(2,1)}, bf16[128,2816]{1,0:T(8,128)(2,1)}, bf16[352,1024]{1,0:T(8,128)(2,1)}, f32[8,128]{1,0:T(8,128)}, bf16[2048,1024]{1,0...) custom-call(bf16[2048,1024]{1,0:T(8,128)(2,1)} %get-tuple-element.44, ...), custom_call_target="tpu_custom_call" | custom-call | tf_op jit(solution)/shard_map/top/pallas_call | solution.py:885
  169.0 83.5 %bottom.1 = (bf16[128,2816]{1,0:T(8,128)(2,1)}, bf16[128,2816]{1,0:T(8,128)(2,1)}, bf16[352,1024]{1,0:T(8,128)(2,1)}, f32[8,128]{1,0:T(8,128)}, bf16[8,32,2816]{...) custom-call(bf16[2048,1024]{1,0:T(8,128)(2,1)} %get-tuple-element.51.refs_0_, bf16[2816,2048]{1,0:T(8,128)(2,1)} %get-tuple-element.52.refs_1_, ...), custom_call_target="tpu_custom_call" | custom-call | tf_op jit(solution)/shard_map/bottom/pallas_call | solution.py:1019
  252.5 145.1 %finish.1 = (bf16[2,1024,2816]{2,1,0:T(8,128)(2,1)S(1)}, bf16[2,1024,2816]{2,1,0:T(8,128)(2,1)S(1)}, bf16[2,2816,1024]{2,1,0:T(8,128)(2,1)S(1)}, f32[2,128,2816]...) custom-call(f32[8,128]{1,0:T(8,128)} %get-tuple-element.58.refs_0_, ...), custom_call_target="tpu_custom_call" | custom-call | tf_op jit(solution)/shard_map/finish/pallas_call | solution.py:348
  397.7 16.7 %store.1 = (bf16[2,1024,2816]{2,1,0:T(8,128)(2,1)}, bf16[2,1024,2816]{2,1,0:T(8,128)(2,1)}, bf16[2,2816,1024]{2,1,0:T(8,128)(2,1)}, f32[2,128,2816]{2,1,0:T(8,12...) custom-call(bf16[2,1024,2816]{2,1,0:T(8,128)(2,1)S(1)} %get-tuple-el, ...), custom_call_target="tpu_custom_call" | custom-call | tf_op jit(solution)/shard_map/store/pallas_call | solution.py:363

commit v4 on v3

--- a/solution.py
+++ b/solution.py
@@ -681,6 +681,16 @@
     return keep
 
 
+def keep_tall(first, down, rows, width, squares):
+    def keep(p, left, right):
+        columns = pl.ds(pl.multiple_of((p - first) * width, width), width)
+        down[:rows, columns] = left
+        down[rows:, columns] = right
+        add_squares(squares, left, right)
+
+    return keep
+
+
 def keep_down(first, down, rows, width, squares):
     def keep(p, left, right):
         half = width // 2
@@ -692,6 +702,16 @@
         add_squares(squares, left, right)
 
     return keep
+
+
+def tall_packet(exchange, step, first, hidden_t, by_out):
+    _, chips, cores, rows, width = exchange.mine.shape
+    half = width // 2
+    by_out = by_out[:, pl.ds(pl.multiple_of((step - first) * half, half), half)]
+    for k in range(chips * cores):
+        block = dot(hidden_t[2 * rows * k : 2 * rows * (k + 1), :], by_out).astype(BF16)
+        for part in range(2):
+            exchange.mine[exchange.held(step), k // cores, k % cores, :, part * half : (part + 1) * half] = block[part * rows : (part + 1) * rows]
 
 
 def down_packet(exchange, step, first, hidden_t, by_out):
@@ -717,8 +737,9 @@
         exchange.mine[exchange.held(step), :, :, pl.ds(0, rows), columns] = block.reshape(chips, cores, rows, half)
 
 
-MB = 512
-LAGS = (0, 1, 3, 5)
+MB = 1024
+TOP_LAGS = (0, 1, 4, 6)
+BOTTOM_LAGS = (0, 1, 4, 7)
 
 
 def top_kernel(n, *refs):
@@ -738,9 +759,9 @@
         n, refs,
         (
             (0, chunks, wide_rows, keep_columns(0, g_gate, g_up, width, squares)),
-            (chunks, chunks + downs, down_rows, keep_down(chunks, g_down, down_rows, 2 * width, squares)),
+            (chunks, chunks + downs, down_rows, keep_tall(chunks, g_down, down_rows, width, squares)),
         ),
-        LAGS,
+        TOP_LAGS,
     )
     layer = w_gate.shape[0] - 1
     first, rest = pl.ds(0, width), pl.ds(width, ff - width)
@@ -843,7 +864,7 @@
 
         @pl.when(t < downs)
         def _():
-            down_packet(exchange, step, chunks, hidden_t, dy)
+            tall_packet(exchange, step, chunks, hidden_t, dy)
 
         exchange.move(step, chunks, chunks + tiles)
         slot = turn(t)
@@ -901,7 +922,7 @@
             *[pltpu.VMEM(t, BF16) for t in ((tokens, d), (d, tokens), (tokens, d), (d, ff), (d, ff), (ff, tokens))],
             *[pltpu.VMEM((BUFFERS, *t), BF16) for t in ((width, d), (tokens, 2 * width), (width, d), (width, d))],
             dma((7,)), dma((BUFFERS,)), dma((2, BUFFERS)), dma((5, BUFFERS)), dma((BUFFERS,)),
-            *Exchange.scratch(n, ff // n // 2, 2 * width, LAGS),
+            *Exchange.scratch(n, ff // n // 2, 2 * width, TOP_LAGS),
         ],
         compiler_params=pltpu.CompilerParams(collective_id=2, has_side_effects=True, vmem_limit_bytes=ALL_VMEM),
         name="top",
@@ -926,7 +947,7 @@
             (0, downs, down_rows, keep_down(0, g_down, down_rows, 2 * width, squares)),
             (downs, downs + chunks, wide_rows, keep_columns(downs, g_gate, g_up, width, squares)),
         ),
-        LAGS,
+        BOTTOM_LAGS,
     )
     share = ff // n
     halves = lambda ref, k: ref.at[:, pl.ds(k * 2 * width, 2 * width)]
@@ -1032,7 +1053,7 @@
             *[pltpu.VMEM(t, BF16) for t in ((tokens, d), (ff, tokens), (d, tokens), (BUFFERS, width, d))],
             *[pltpu.VMEM((BUFFERS, tokens, width), F32)] * 2, pltpu.VMEM((tokens, 2 * width), BF16),
             dma((3 + 2 * n,)), dma((3, BUFFERS)),
-            *Exchange.scratch(n, ff // n // 2, 2 * width, LAGS),
+            *Exchange.scratch(n, ff // n // 2, 2 * width, BOTTOM_LAGS),
         ],
         compiler_params=pltpu.CompilerParams(collective_id=3, has_side_effects=True, vmem_limit_bytes=ALL_VMEM),
         name="bottom",

time: 415 us -> 413 us (level)
  no operation moved by 1% of the time
where the time goes in v4:
time: 413 us
  Pallas kernels  412 us (100%)
    pallas_call x1, Pallas kernels, finish(): pl.pallas_call(functools.partial(finish_kernel, n, count, layers, tuple(p...  144 us
    pallas_call x1, Pallas kernels, top_layer(): pl.pallas_call(functools.partial(top_kernel, n), in_specs=[anywhere] * (7...  120 us
    pallas_call x1, Pallas kernels, bottom_layer(): pl.pallas_call(functools.partial(bottom_kernel, n), in_specs=[anywhere] *...  83.5 us
    pallas_call x1, Pallas kernels, layer_0(): pl.pallas_call(functools.partial(forward_kernel, n), in_specs=[anywhere]...  47 us
    pallas_call x1, Pallas kernels, finish(): pl.pallas_call(store_kernel, out_shape=[jax.ShapeDtypeStruct(t.shape, t.d...  16.7 us

profile of v4, /device:TPU:113, one launch (start us, length us, event | category | flops | bytes accessed | tf_op | source)
XLA Modules:
  0.0 412.8 jit_solution(14371171734151202783)
XLA Ops:
  0.6 47.0 %forward.1 = (f32[2048,2816]{1,0:T(8,128)}, f32[2048,2816]{1,0:T(8,128)}, bf16[2816,2048]{1,0:T(8,128)(2,1)}, bf16[1024,2048]{1,0:T(8,128)(2,1)}, bf16[2048,1024...) custom-call(bf16[2048,1024]{1,0:T(8,128)(2,1)} %bitcast.2, ...), custom_call_target="tpu_custom_call" | custom-call | tf_op jit(solution)/shard_map/forward/pallas_call | solution.py:518
  47.6 120.3 %top.1 = (bf16[128,2816]{1,0:T(8,128)(2,1)}, bf16[128,2816]{1,0:T(8,128)(2,1)}, bf16[352,1024]{1,0:T(8,128)(2,1)}, f32[8,128]{1,0:T(8,128)}, bf16[2048,1024]{1,0...) custom-call(bf16[2048,1024]{1,0:T(8,128)(2,1)} %get-tuple-element.44, ...), custom_call_target="tpu_custom_call" | custom-call | tf_op jit(solution)/shard_map/top/pallas_call | solution.py:906
  167.9 83.5 %bottom.1 = (bf16[128,2816]{1,0:T(8,128)(2,1)}, bf16[128,2816]{1,0:T(8,128)(2,1)}, bf16[352,1024]{1,0:T(8,128)(2,1)}, f32[8,128]{1,0:T(8,128)}, bf16[8,32,2816]{...) custom-call(bf16[2048,1024]{1,0:T(8,128)(2,1)} %get-tuple-element.51.refs_0_, bf16[2816,2048]{1,0:T(8,128)(2,1)} %get-tuple-element.52.refs_1_, ...), custom_call_target="tpu_custom_call" | custom-call | tf_op jit(solution)/shard_map/bottom/pallas_call | solution.py:1040
  251.4 144.4 %finish.1 = (bf16[2,1024,2816]{2,1,0:T(8,128)(2,1)S(1)}, bf16[2,1024,2816]{2,1,0:T(8,128)(2,1)S(1)}, bf16[2,2816,1024]{2,1,0:T(8,128)(2,1)S(1)}, f32[2,128,2816]...) custom-call(f32[8,128]{1,0:T(8,128)} %get-tuple-element.58.refs_0_, ...), custom_call_target="tpu_custom_call" | custom-call | tf_op jit(solution)/shard_map/finish/pallas_call | solution.py:348
  395.9 16.7 %store.1 = (bf16[2,1024,2816]{2,1,0:T(8,128)(2,1)}, bf16[2,1024,2816]{2,1,0:T(8,128)(2,1)}, bf16[2,2816,1024]{2,1,0:T(8,128)(2,1)}, f32[2,128,2816]{2,1,0:T(8,12...) custom-call(bf16[2,1024,2816]{2,1,0:T(8,128)(2,1)S(1)} %get-tuple-el, ...), custom_call_target="tpu_custom_call" | custom-call | tf_op jit(solution)/shard_map/store/pallas_call | solution.py:363

commit v5 on v4

--- a/solution.py
+++ b/solution.py
@@ -301,10 +301,11 @@
             for k in range(min(3, len(units) - done)):
                 unit(done + k)
             done += min(3, len(units) - done)
+        if number == 3:
+            for i, some in EARLY:
+                compute(i, last, g[i].shape[1] - some, some)
     for k in range(done, len(units)):
         unit(k)
-    for i, some in EARLY:
-        compute(i, last, g[i].shape[1] - some, some)
     for copies in made:
         spread.end(copies)
     for one in part_copies:
@@ -321,8 +322,8 @@
         one.wait()
 
 
-def early_shapes(n, blocks, dtype, times=1):
-    return [jax.ShapeDtypeStruct((n, some, blocks[i][0].shape[-1]), dtype) for _ in range(times) for i, some in EARLY]
+def early_shapes(n, blocks, dtype, times=1, kind=jax.ShapeDtypeStruct):
+    return [kind((n, some, blocks[i][0].shape[-1]), dtype) for _ in range(times) for i, some in EARLY]
 
 
 def finish(n, gradients, squares, weights, m, v, early):
@@ -338,7 +339,7 @@
                 cuts = [48, half - 48, half]
             elif layer == layers - 1 and i in dict(EARLY):
                 rest = half - dict(EARLY)[i]
-                cuts = [half, rest - 16, 16] if i == 1 else [half, rest]
+                cuts = [half + rest - 16, 16] if i == 1 else [half + rest]
             for cut in cuts:
                 pieces.append((i, layer, sum(p[3] for p in pieces if p[:2] == (i, layer)), cut))
     anywhere, inside = pl.BlockSpec(memory_space=pl.ANY), pl.BlockSpec(memory_space=pltpu.VMEM)
@@ -520,23 +521,23 @@
         in_specs=[anywhere] * (4 + 2 * len(EARLY)),
         out_specs=[anywhere] * (7 + 2 * len(EARLY)),
         out_shape=[
-            jax.ShapeDtypeStruct((tokens, ff), F32),
-            jax.ShapeDtypeStruct((tokens, ff), F32),
-            jax.ShapeDtypeStruct((ff, tokens), BF16),
-            jax.ShapeDtypeStruct((d, tokens), BF16),
-            jax.ShapeDtypeStruct((tokens, d), BF16),
-            jax.ShapeDtypeStruct((tokens, d), BF16),
-            jax.ShapeDtypeStruct((d, tokens), BF16),
-            *early_shapes(n, m, F32, 2),
+            pltpu.HBM((tokens, ff), F32),
+            pltpu.HBM((tokens, ff), F32),
+            pltpu.HBM((ff, tokens), BF16),
+            pltpu.HBM((d, tokens), BF16),
+            pltpu.HBM((tokens, d), BF16),
+            pltpu.HBM((tokens, d), BF16),
+            pltpu.HBM((d, tokens), BF16),
+            *early_shapes(n, m, F32, 2, pltpu.HBM),
         ],
         scratch_shapes=[
             vmem(d, ff), vmem(d, ff), vmem(ff, d), vmem(rows, ff), vmem(3, rows, d),
             *[pltpu.VMEM((BUFFERS, rows, ff), F32)] * 2, *[vmem(BUFFERS, *t) for t in ((ff, rows), (d, rows), (rows, d), (rows, d), (d, rows))],
             dma((WEIGHTS, 4)), dma((3,)), dma((4, BUFFERS)), dma((3, BUFFERS)), *Spread.semaphores(2 * len(EARLY)),
         ],
-        compiler_params=pltpu.CompilerParams(collective_id=1, has_side_effects=True, vmem_limit_bytes=60 * MIB),
+        compiler_params=pltpu.CompilerParams(collective_id=1, has_side_effects=True, vmem_limit_bytes=48 * MIB),
         name="forward",
-    )(x, w_gate, w_up, w_down, *[t[i] for t in (m, v) for i, _ in EARLY])
+    )(*[pltpu.with_memory_space_constraint(t, pltpu.HBM) for t in (x, w_gate, w_up, w_down, *[t[i] for t in (m, v) for i, _ in EARLY])])
 
 
 class Exchange:
@@ -745,10 +746,10 @@
 def top_kernel(n, *refs):
     several = 2 * len(EARLY)
     ins, near, outs, far, (send, recv), refs = split(refs, 7, several, 7, several, 2)
-    a_in, at_in, h_in, dy_in, w_gate, w_up, w_down = ins
+    a_in, at_in, h_in, dy, w_gate, w_up, w_down = ins
     g_gate, g_up, g_down, squares, by_h, bg_hbm, bu_hbm = outs
     spread = Spread(n, send, recv)
-    (a, a_t, dy, wg, wu, hidden_t, wd, both, h_tile, by_tile, load_sem, wd_sem, both_sem, tile_sem, by_sem), refs = split(refs, 15)
+    (a, a_t, wg, wu, hidden_t, wd, both, h_tile, by_tile, load_sem, wd_sem, both_sem, tile_sem, by_sem), refs = split(refs, 14)
     tokens, d = a.shape
     ff = wg.shape[1]
     width = 256
@@ -766,12 +767,12 @@
     layer = w_gate.shape[0] - 1
     first, rest = pl.ds(0, width), pl.ds(width, ff - width)
     columns_of = lambda columns: [(src.at[layer, :, columns], dst.at[:, columns]) for src, dst in ((w_gate, wg), (w_up, wu))]
-    loads = local_copies([(a_in, a), (dy_in, dy), (at_in, a_t), *columns_of(first), *columns_of(rest)], load_sem)
+    loads = local_copies([(a_in, a), (at_in, a_t), *columns_of(first), *columns_of(rest)], load_sem)
     def down_chunk(c):
         slot = turn(c)
         return pltpu.make_async_copy(w_down.at[layer, pl.ds(pl.multiple_of(c * width, width), width)], wd.at[slot], wd_sem.at[slot])
 
-    loads, later_loads = split(loads, 5)
+    loads, later_loads = split(loads, 4)
     for one in (*loads, down_chunk(0)):
         one.start()
     squares[...] = jnp.zeros_like(squares)
@@ -905,7 +906,7 @@
     dma = pltpu.SemaphoreType.DMA
     return pl.pallas_call(
         functools.partial(top_kernel, n),
-        in_specs=[anywhere] * (7 + len(near)),
+        in_specs=[*[anywhere] * 3, inside, *[anywhere] * (3 + len(near))],
         out_specs=[inside] * 4 + [anywhere] * (3 + len(near)),
         out_shape=[
             jax.ShapeDtypeStruct((d // n, ff), BF16),
@@ -919,14 +920,14 @@
         ],
         scratch_shapes=[
             *Spread.semaphores(len(near)),
-            *[pltpu.VMEM(t, BF16) for t in ((tokens, d), (d, tokens), (tokens, d), (d, ff), (d, ff), (ff, tokens))],
+            *[pltpu.VMEM(t, BF16) for t in ((tokens, d), (d, tokens), (d, ff), (d, ff), (ff, tokens))],
             *[pltpu.VMEM((BUFFERS, *t), BF16) for t in ((width, d), (tokens, 2 * width), (width, d), (width, d))],
-            dma((7,)), dma((BUFFERS,)), dma((2, BUFFERS)), dma((5, BUFFERS)), dma((BUFFERS,)),
+            dma((6,)), dma((BUFFERS,)), dma((2, BUFFERS)), dma((5, BUFFERS)), dma((BUFFERS,)),
             *Exchange.scratch(n, ff // n // 2, 2 * width, TOP_LAGS),
         ],
-        compiler_params=pltpu.CompilerParams(collective_id=2, has_side_effects=True, vmem_limit_bytes=ALL_VMEM),
+        compiler_params=pltpu.CompilerParams(collective_id=2, has_side_effects=True, vmem_limit_bytes=ALL_VMEM - 9 * MIB // 2),
         name="top",
-    )(a, a_t, h, dy, w_gate, w_up, w_down, *near)
+    )(a, a_t, h, pltpu.with_memory_space_constraint(dy, pltpu.VMEM), w_gate, w_up, w_down, *near)
 
 
 def bottom_kernel(n, *refs):

time: 413 us -> 410 us (level)
  no operation moved by 1% of the time
where the time goes in v5:
time: 410 us
  Pallas kernels  409 us (100%)
    pallas_call x1, Pallas kernels, finish(): pl.pallas_call(functools.partial(finish_kernel, n, count, layers, tuple(p...  142 us
    pallas_call x1, Pallas kernels, top_layer(): pl.pallas_call(functools.partial(top_kernel, n), in_specs=[*[anywhere] *...  120 us
    pallas_call x1, Pallas kernels, bottom_layer(): pl.pallas_call(functools.partial(bottom_kernel, n), in_specs=[anywhere] *...  83.5 us
    pallas_call x1, Pallas kernels, layer_0(): pl.pallas_call(functools.partial(forward_kernel, n), in_specs=[anywhere]...  47 us
    pallas_call x1, Pallas kernels, finish(): pl.pallas_call(store_kernel, out_shape=[jax.ShapeDtypeStruct(t.shape, t.d...  16.7 us

profile of v5, /device:TPU:113, one launch (start us, length us, event | category | flops | bytes accessed | tf_op | source)
XLA Modules:
  0.0 409.8 jit_solution(6440690074318654838)
XLA Ops:
  0.6 0.0 copy-start
  0.7 47.0 %forward.1 = (f32[2048,2816]{1,0:T(8,128)}, f32[2048,2816]{1,0:T(8,128)}, bf16[2816,2048]{1,0:T(8,128)(2,1)}, bf16[1024,2048]{1,0:T(8,128)(2,1)}, bf16[2048,1024...) custom-call(bf16[2048,1024]{1,0:T(8,128)(2,1)} %bitcast.3, ...), custom_call_target="tpu_custom_call" | custom-call | tf_op jit(solution)/shard_map/forward/pallas_call | solution.py:519
  47.7 0.0 copy-done
  47.7 119.7 %top.1 = (bf16[128,2816]{1,0:T(8,128)(2,1)}, bf16[128,2816]{1,0:T(8,128)(2,1)}, bf16[352,1024]{1,0:T(8,128)(2,1)}, f32[8,128]{1,0:T(8,128)}, bf16[2048,1024]{1,0...) custom-call(bf16[2048,1024]{1,0:T(8,128)(2,1)} %get-tuple-element.44, ...), custom_call_target="tpu_custom_call" | custom-call | tf_op jit(solution)/shard_map/top/pallas_call | solution.py:907
  167.4 83.5 %bottom.1 = (bf16[128,2816]{1,0:T(8,128)(2,1)}, bf16[128,2816]{1,0:T(8,128)(2,1)}, bf16[352,1024]{1,0:T(8,128)(2,1)}, f32[8,128]{1,0:T(8,128)}, bf16[8,32,2816]{...) custom-call(bf16[2048,1024]{1,0:T(8,128)(2,1)} %get-tuple-element.51.refs_0_, bf16[2816,2048]{1,0:T(8,128)(2,1)} %get-tuple-element.52.refs_1_, ...), custom_call_target="tpu_custom_call" | custom-call | tf_op jit(solution)/shard_map/bottom/pallas_call | solution.py:1041
  250.9 142.0 %finish.1 = (bf16[2,1024,2816]{2,1,0:T(8,128)(2,1)S(1)}, bf16[2,1024,2816]{2,1,0:T(8,128)(2,1)S(1)}, bf16[2,2816,1024]{2,1,0:T(8,128)(2,1)S(1)}, f32[2,128,2816]...) custom-call(f32[8,128]{1,0:T(8,128)} %get-tuple-element.58.refs_0_, ...), custom_call_target="tpu_custom_call" | custom-call | tf_op jit(solution)/shard_map/finish/pallas_call | solution.py:349
  392.9 16.7 %store.1 = (bf16[2,1024,2816]{2,1,0:T(8,128)(2,1)}, bf16[2,1024,2816]{2,1,0:T(8,128)(2,1)}, bf16[2,2816,1024]{2,1,0:T(8,128)(2,1)}, f32[2,128,2816]{2,1,0:T(8,12...) custom-call(bf16[2,1024,2816]{2,1,0:T(8,128)(2,1)S(1)} %get-tuple-el, ...), custom_call_target="tpu_custom_call" | custom-call | tf_op jit(solution)/shard_map/store/pallas_call | solution.py:364
Async XLA Ops:
  0.6 47.1 %copy-start = (bf16[1,2048,1024]{2,1,0:T(8,128)(2,1)S(1)}, bf16[1,2048,1024]{2,1,0:T(8,128)(2,1)}, u32[]{:S(2)}) copy-start(bf16[1,2048,1024]{2,1,0:T(8,128)(2,1)} %param.12) | copy-start | bytes 12582916

commit v6 on v5

--- a/solution.py
+++ b/solution.py
@@ -650,7 +650,8 @@
             self.move(step, step, step + 1)
 
     def move(self, step, low, high):
-        for lag, stage in zip(self.lags, (self.stage1, self.stage2, self.stage3, self.stage4), strict=True):
+        one, two, three, four = zip(self.lags, (self.stage1, self.stage2, self.stage3, self.stage4), strict=True)
+        for lag, stage in (one, three, two, four):
             for first, end, rows, keep in self.kinds:
                 if high - 1 - lag < first or low - lag >= end:
                     continue
@@ -740,7 +741,7 @@
 
 MB = 1024
 TOP_LAGS = (0, 1, 4, 6)
-BOTTOM_LAGS = (0, 1, 4, 7)
+BOTTOM_LAGS = (0, 1, 5, 9)
 
 
 def top_kernel(n, *refs):

time: 410 us -> 408 us (level)
  no operation moved by 1% of the time
where the time goes in v6:
time: 408 us
  Pallas kernels  407 us (100%)
    pallas_call x1, Pallas kernels, finish(): pl.pallas_call(functools.partial(finish_kernel, n, count, layers, tuple(p...  141 us
    pallas_call x1, Pallas kernels, top_layer(): pl.pallas_call(functools.partial(top_kernel, n), in_specs=[*[anywhere] *...  118 us
    pallas_call x1, Pallas kernels, bottom_layer(): pl.pallas_call(functools.partial(bottom_kernel, n), in_specs=[anywhere] *...  84.4 us
    pallas_call x1, Pallas kernels, layer_0(): pl.pallas_call(functools.partial(forward_kernel, n), in_specs=[anywhere]...  47 us
    pallas_call x1, Pallas kernels, finish(): pl.pallas_call(store_kernel, out_shape=[jax.ShapeDtypeStruct(t.shape, t.d...  16.7 us

profile of v6, /device:TPU:113, one launch (start us, length us, event | category | flops | bytes accessed | tf_op | source)
XLA Modules:
  0.0 408.1 jit_solution(16156406465130123538)
XLA Ops:
  0.6 0.0 copy-start
  0.7 47.0 %forward.1 = (f32[2048,2816]{1,0:T(8,128)}, f32[2048,2816]{1,0:T(8,128)}, bf16[2816,2048]{1,0:T(8,128)(2,1)}, bf16[1024,2048]{1,0:T(8,128)(2,1)}, bf16[2048,1024...) custom-call(bf16[2048,1024]{1,0:T(8,128)(2,1)} %bitcast.3, ...), custom_call_target="tpu_custom_call" | custom-call | tf_op jit(solution)/shard_map/forward/pallas_call | solution.py:519
  47.7 0.0 copy-done
  47.7 117.8 %top.1 = (bf16[128,2816]{1,0:T(8,128)(2,1)}, bf16[128,2816]{1,0:T(8,128)(2,1)}, bf16[352,1024]{1,0:T(8,128)(2,1)}, f32[8,128]{1,0:T(8,128)}, bf16[2048,1024]{1,0...) custom-call(bf16[2048,1024]{1,0:T(8,128)(2,1)} %get-tuple-element.44, ...), custom_call_target="tpu_custom_call" | custom-call | tf_op jit(solution)/shard_map/top/pallas_call | solution.py:908
  165.6 84.4 %bottom.1 = (bf16[128,2816]{1,0:T(8,128)(2,1)}, bf16[128,2816]{1,0:T(8,128)(2,1)}, bf16[352,1024]{1,0:T(8,128)(2,1)}, f32[8,128]{1,0:T(8,128)}, bf16[8,32,2816]{...) custom-call(bf16[2048,1024]{1,0:T(8,128)(2,1)} %get-tuple-element.51.refs_0_, bf16[2816,2048]{1,0:T(8,128)(2,1)} %get-tuple-element.52.refs_1_, ...), custom_call_target="tpu_custom_call" | custom-call | tf_op jit(solution)/shard_map/bottom/pallas_call | solution.py:1042
  250.0 141.2 %finish.1 = (bf16[2,1024,2816]{2,1,0:T(8,128)(2,1)S(1)}, bf16[2,1024,2816]{2,1,0:T(8,128)(2,1)S(1)}, bf16[2,2816,1024]{2,1,0:T(8,128)(2,1)S(1)}, f32[2,128,2816]...) custom-call(f32[8,128]{1,0:T(8,128)} %get-tuple-element.58.refs_0_, ...), custom_call_target="tpu_custom_call" | custom-call | tf_op jit(solution)/shard_map/finish/pallas_call | solution.py:349
  391.2 16.7 %store.1 = (bf16[2,1024,2816]{2,1,0:T(8,128)(2,1)}, bf16[2,1024,2816]{2,1,0:T(8,128)(2,1)}, bf16[2,2816,1024]{2,1,0:T(8,128)(2,1)}, f32[2,128,2816]{2,1,0:T(8,12...) custom-call(bf16[2,1024,2816]{2,1,0:T(8,128)(2,1)S(1)} %get-tuple-el, ...), custom_call_target="tpu_custom_call" | custom-call | tf_op jit(solution)/shard_map/store/pallas_call | solution.py:364
Async XLA Ops:
  0.6 47.1 %copy-start = (bf16[1,2048,1024]{2,1,0:T(8,128)(2,1)S(1)}, bf16[1,2048,1024]{2,1,0:T(8,128)(2,1)}, u32[]{:S(2)}) copy-start(bf16[1,2048,1024]{2,1,0:T(8,128)(2,1)} %param.12) | copy-start | bytes 12582916

commit v7 on v6

--- a/solution.py
+++ b/solution.py
@@ -315,7 +315,7 @@
 def store_kernel(*refs):
     *refs, sem = refs
     some = len(refs) // 2
-    copies = local_copies([(refs[k], refs[some + k]) for k in range(some)], sem)
+    copies = local_copies([(refs[k].at[layer], refs[some + k].at[layer]) for layer in range(refs[0].shape[0]) for k in range(some)], sem)
     for one in copies:
         one.start()
     for one in copies:
@@ -366,7 +366,7 @@
         out_shape=[jax.ShapeDtypeStruct(t.shape, t.dtype) for t in results],
         in_specs=[inside] * len(results),
         out_specs=[anywhere] * len(results),
-        scratch_shapes=[dma((len(results),))],
+        scratch_shapes=[dma((len(results) * layers,))],
         compiler_params=pltpu.CompilerParams(vmem_limit_bytes=8 * MIB),
         name="store",
     )(*[pltpu.with_memory_space_constraint(t, pltpu.VMEM) for t in ready])

time: 408 us -> 408 us (level)
  no operation moved by 1% of the time
where the time goes in v7:
time: 408 us
  Pallas kernels  407 us (100%)
    pallas_call x1, Pallas kernels, finish(): pl.pallas_call(functools.partial(finish_kernel, n, count, layers, tuple(p...  141 us
    pallas_call x1, Pallas kernels, top_layer(): pl.pallas_call(functools.partial(top_kernel, n), in_specs=[*[anywhere] *...  118 us
    pallas_call x1, Pallas kernels, bottom_layer(): pl.pallas_call(functools.partial(bottom_kernel, n), in_specs=[anywhere] *...  84.4 us
    pallas_call x1, Pallas kernels, layer_0(): pl.pallas_call(functools.partial(forward_kernel, n), in_specs=[anywhere]...  47 us
    pallas_call x1, Pallas kernels, finish(): pl.pallas_call(store_kernel, out_shape=[jax.ShapeDtypeStruct(t.shape, t.d...  16.6 us

profile of v7, /device:TPU:113, one launch (start us, length us, event | category | flops | bytes accessed | tf_op | source)
XLA Modules:
  0.0 408.0 jit_solution(2097206557666646779)
XLA Ops:
  0.6 0.0 copy-start
  0.7 47.0 %forward.1 = (f32[2048,2816]{1,0:T(8,128)}, f32[2048,2816]{1,0:T(8,128)}, bf16[2816,2048]{1,0:T(8,128)(2,1)}, bf16[1024,2048]{1,0:T(8,128)(2,1)}, bf16[2048,1024...) custom-call(bf16[2048,1024]{1,0:T(8,128)(2,1)} %bitcast.3, ...), custom_call_target="tpu_custom_call" | custom-call | tf_op jit(solution)/shard_map/forward/pallas_call | solution.py:519
  47.7 0.0 copy-done
  47.7 117.8 %top.1 = (bf16[128,2816]{1,0:T(8,128)(2,1)}, bf16[128,2816]{1,0:T(8,128)(2,1)}, bf16[352,1024]{1,0:T(8,128)(2,1)}, f32[8,128]{1,0:T(8,128)}, bf16[2048,1024]{1,0...) custom-call(bf16[2048,1024]{1,0:T(8,128)(2,1)} %get-tuple-element.44, ...), custom_call_target="tpu_custom_call" | custom-call | tf_op jit(solution)/shard_map/top/pallas_call | solution.py:908
  165.6 84.4 %bottom.1 = (bf16[128,2816]{1,0:T(8,128)(2,1)}, bf16[128,2816]{1,0:T(8,128)(2,1)}, bf16[352,1024]{1,0:T(8,128)(2,1)}, f32[8,128]{1,0:T(8,128)}, bf16[8,32,2816]{...) custom-call(bf16[2048,1024]{1,0:T(8,128)(2,1)} %get-tuple-element.51.refs_0_, bf16[2816,2048]{1,0:T(8,128)(2,1)} %get-tuple-element.52.refs_1_, ...), custom_call_target="tpu_custom_call" | custom-call | tf_op jit(solution)/shard_map/bottom/pallas_call | solution.py:1042
  250.0 141.2 %finish.1 = (bf16[2,1024,2816]{2,1,0:T(8,128)(2,1)S(1)}, bf16[2,1024,2816]{2,1,0:T(8,128)(2,1)S(1)}, bf16[2,2816,1024]{2,1,0:T(8,128)(2,1)S(1)}, f32[2,128,2816]...) custom-call(f32[8,128]{1,0:T(8,128)} %get-tuple-element.58.refs_0_, ...), custom_call_target="tpu_custom_call" | custom-call | tf_op jit(solution)/shard_map/finish/pallas_call | solution.py:349
  391.2 16.6 %store.1 = (bf16[2,1024,2816]{2,1,0:T(8,128)(2,1)}, bf16[2,1024,2816]{2,1,0:T(8,128)(2,1)}, bf16[2,2816,1024]{2,1,0:T(8,128)(2,1)}, f32[2,128,2816]{2,1,0:T(8,12...) custom-call(bf16[2,1024,2816]{2,1,0:T(8,128)(2,1)S(1)} %get-tuple-el, ...), custom_call_target="tpu_custom_call" | custom-call | tf_op jit(solution)/shard_map/store/pallas_call | solution.py:364
Async XLA Ops:
  0.6 47.1 %copy-start = (bf16[1,2048,1024]{2,1,0:T(8,128)(2,1)S(1)}, bf16[1,2048,1024]{2,1,0:T(8,128)(2,1)}, u32[]{:S(2)}) copy-start(bf16[1,2048,1024]{2,1,0:T(8,128)(2,1)} %param.12) | copy-start | bytes 12582916
